TPU v7x, 128 devices: a whole 4x4x4 slice. The times are simulated.
128 devices in a mesh: band: 16 (over x, y), tm: 8 (over z, core).
Axes of the slice: x: 4, y: 4, z: 4, core: 2. Of those that a mesh axis runs over, the one named last changes fastest.
Arguments:
- spec: bfloat16 [2048, 4096], P('tm', 'band'), may hold values from -6 to 6
- cotangent: bfloat16 [2048, 4096], P('tm', 'band'), may hold values from -0.29882812 to 0.29882812
- widths: int32 [32], replicated, may hold values from 16 to 64, as said below
- band_group: int32 [32], replicated, may hold values from 0 to 15, as said below
- w_embed: bfloat16 [256, 64, 384], P(None, 'band'), may hold values from -0.375 to 0.375
- w_qkv: bfloat16 [384, 1536], replicated, may hold values from -2 to 2
- w_proj: bfloat16 [512, 384], replicated, may hold values from -0.25 to 0.25
- w_hidden: bfloat16 [384, 64, 1536], P(None, 'band'), may hold values from -0.3125 to 0.3125
- w_out: bfloat16 [1536, 64, 512], P(None, 'band'), may hold values from -0.15625 to 0.15625
Outputs:
- mask: bfloat16 [2048, 4096], P('tm', 'band')
- grad_embed: bfloat16 [256, 64, 384], P('tm', 'band')
- grad_qkv: float32 [384, 1536], replicated
- grad_proj: float32 [512, 384], replicated
- grad_hidden: bfloat16 [384, 64, 1536], P('tm', 'band')
- grad_out: bfloat16 [1536, 64, 512], P('tm', 'band')
Inputs may be any that keep to these rules, and one draw needn't show every extreme that they name: The widths sum to 1024 and at least one band has exactly 64 bins. `band_group`: every group owns at most 4 bands, and some group owns exactly 4.
All inputs are finite; a program needn't handle non-finite values.
Results may differ from a plain program's by a relative error of at most 0.02.
Values may be sent and summed in bfloat16 or wider, within the bound.
A program may use at most 128 MiB of HBM per device.

v0:
```python
import jax
import jax.numpy as jnp
from jax import lax
from jax.sharding import Mesh
from jax.sharding import PartitionSpec as P

HEAD_DIM = 64
BAND = ("band_0", "band_1")
BAND_TM = ("band_0", "band_1", "tm")


EPSILON = 1e-05


def cut_along(shard, dim, peers):
    lengths = shard.shape
    pieces = shard.reshape(*lengths[:dim], peers, lengths[dim] // peers, *lengths[dim + 1 :])
    return jnp.moveaxis(pieces, dim, 0)


def sent_and_summed(shard, axis, dim):
    peers = lax.axis_size(axis)
    pieces = lax.all_to_all(cut_along(shard, dim, peers), axis, 0, 0, tiled=True)
    return jnp.sum(pieces.astype(jnp.float32), axis=0)


def in_one_piece(arrays, axis, dim, along):
    widths = [a.shape[along] for a in arrays]
    both = jnp.concatenate(arrays, axis=along)
    out = lax.all_gather(both, axis, axis=dim, tiled=True)
    return tuple(jnp.split(out, [sum(widths[:k]) for k in range(1, len(widths))], axis=along))


def summed_rows(shard, axes, dim):
    for axis in axes:
        shard = lax.psum_scatter(shard, axis, scatter_dimension=dim, tiled=True)
    return shard


def packed_total(arrays, axis):
    ends = [0]
    for a in arrays:
        ends.append(ends[-1] + a.size)
    subtotal = lax.psum(jnp.concatenate([a.ravel() for a in arrays]), axis)
    return tuple((subtotal[b:e].reshape(a.shape) for a, b, e in zip(arrays, ends, ends[1:])))


def row_norm(values):
    inv_rms = lax.rsqrt(jnp.mean(values * values, axis=-1, keepdims=True) + EPSILON)
    return (values * inv_rms, inv_rms)


def attention_forward(tokens, key_valid, w_qkv, w_proj):
    inner_width = w_proj.shape[0]
    head_count = inner_width // HEAD_DIM
    rows, width_k = (tokens.shape[0], tokens.shape[1])
    token32 = tokens.astype(jnp.float32)
    normed32, inv_rms = row_norm(token32)
    normed = normed32.astype(jnp.bfloat16)
    packed = jnp.einsum("nkd,de->nke", normed, w_qkv, preferred_element_type=jnp.float32).astype(
        jnp.bfloat16
    )
    queries = packed[:, :, :inner_width].reshape(rows, width_k, head_count, HEAD_DIM)
    key_rows = packed[:, :, inner_width : 2 * inner_width].reshape(
        rows, width_k, head_count, HEAD_DIM
    )
    value_rows = packed[:, :, 2 * inner_width :].reshape(rows, width_k, head_count, HEAD_DIM)
    scores = jnp.einsum(
        "nqhc,nkhc->nhqk", queries, key_rows, preferred_element_type=jnp.float32
    ) * HEAD_DIM ** (-0.5)
    scores = jnp.where(key_valid[None, None, None, :], scores, -jnp.inf)
    highest = jnp.max(scores, axis=-1, keepdims=True)
    expd = jnp.exp(scores - highest)
    soft_weights = expd / jnp.sum(expd, axis=-1, keepdims=True)
    soft_rounded = soft_weights.astype(jnp.bfloat16)
    heads_out = jnp.einsum(
        "nhqk,nkhc->nqhc", soft_rounded, value_rows, preferred_element_type=jnp.float32
    )
    heads_out = heads_out.astype(jnp.bfloat16).reshape(rows, width_k, inner_width)
    result = token32 + jnp.einsum(
        "nki,id->nkd", heads_out, w_proj, preferred_element_type=jnp.float32
    )
    saved = (
        normed32,
        inv_rms,
        normed,
        queries,
        key_rows,
        value_rows,
        soft_weights,
        soft_rounded,
        heads_out,
    )
    return (result.astype(jnp.bfloat16), saved)


def attention_backward(saved, grad_out, w_qkv, w_proj):
    (
        normed32,
        inv_rms,
        normed,
        queries,
        key_rows,
        value_rows,
        soft_weights,
        soft_rounded,
        heads_out,
    ) = saved
    inner_width = w_proj.shape[0]
    head_count = inner_width // HEAD_DIM
    rows, width_k = (grad_out.shape[0], grad_out.shape[1])
    grad32 = grad_out.astype(jnp.float32)
    grad_proj = jnp.einsum("nki,nkd->id", heads_out, grad_out, preferred_element_type=jnp.float32)
    grad_heads = jnp.einsum(
        "nkd,id->nki", grad_out, w_proj, preferred_element_type=jnp.float32
    ).astype(jnp.bfloat16)
    grad_heads = grad_heads.reshape(rows, width_k, head_count, HEAD_DIM)
    grad_soft = jnp.einsum(
        "nqhc,nkhc->nhqk", grad_heads, value_rows, preferred_element_type=jnp.float32
    )
    grad_values = jnp.einsum(
        "nhqk,nqhc->nkhc", soft_rounded, grad_heads, preferred_element_type=jnp.float32
    )
    grad_scores = soft_weights * (
        grad_soft - jnp.sum(grad_soft * soft_weights, axis=-1, keepdims=True)
    )
    grad_scores = (grad_scores * HEAD_DIM ** (-0.5)).astype(jnp.bfloat16)
    grad_queries = jnp.einsum(
        "nhqk,nkhc->nqhc", grad_scores, key_rows, preferred_element_type=jnp.float32
    )
    grad_keys = jnp.einsum(
        "nhqk,nqhc->nkhc", grad_scores, queries, preferred_element_type=jnp.float32
    )
    grad_packed = jnp.concatenate(
        [
            grad_queries.reshape(rows, width_k, inner_width),
            grad_keys.reshape(rows, width_k, inner_width),
            grad_values.reshape(rows, width_k, inner_width),
        ],
        axis=-1,
    ).astype(jnp.bfloat16)
    grad_qkv = jnp.einsum("nkd,nke->de", normed, grad_packed, preferred_element_type=jnp.float32)
    grad_normed = jnp.einsum("nke,de->nkd", grad_packed, w_qkv, preferred_element_type=jnp.float32)
    grad_tokens = grad32 + inv_rms * (
        grad_normed - normed32 * jnp.mean(grad_normed * normed32, axis=-1, keepdims=True)
    )
    return (grad_tokens.astype(jnp.bfloat16), grad_qkv, grad_proj)


def weight_grad(left, right):
    return sent_and_summed(
        jnp.einsum("fsa,fsb->asb", left, right, preferred_element_type=jnp.float32).astype(
            jnp.bfloat16
        ),
        "tm",
        0,
    )


def per_device(spec, cotangent, widths, band_group, w_embed, w_qkv, w_proj, w_hidden, w_out):
    frame_count = spec.shape[0]
    feat = w_embed.shape[0]
    slot_count = w_embed.shape[1]
    group_count = lax.axis_size(BAND)
    group_index = lax.axis_index(BAND)
    band_count = widths.shape[0]
    starts = jnp.cumsum(widths) - widths
    positions = jnp.arange(band_count)
    same_group = band_group[:, None] == band_group[None, :]
    earlier = positions[None, :] < positions[:, None]
    ranks = jnp.sum(jnp.where(same_group & earlier, 1, 0), axis=1).astype(jnp.int32)
    own_slots = (band_group[None, :] == group_index) & (
        ranks[None, :] == jnp.arange(slot_count)[:, None]
    )
    slot_start = jnp.sum(jnp.where(own_slots, starts[None, :], 0), axis=1)
    slot_width = jnp.sum(jnp.where(own_slots, widths[None, :], 0), axis=1)
    global_slot = band_group * slot_count + ranks
    holder = global_slot[None, :] == jnp.arange(group_count * slot_count)[:, None]
    spec_full, cot_full = in_one_piece((spec, cotangent), BAND, 1, 0)
    bins_total = spec_full.shape[1]
    spec_pad = jnp.pad(spec_full, ((0, 0), (0, feat)))
    cot_pad = jnp.pad(cot_full, ((0, 0), (0, feat)))
    spec_tiles = jnp.stack(
        [
            lax.dynamic_slice_in_dim(spec_pad, 4 * slot_start[slot_id], feat, 1)
            for slot_id in range(slot_count)
        ],
        axis=1,
    )
    cot_tiles = jnp.stack(
        [
            lax.dynamic_slice_in_dim(cot_pad, 4 * slot_start[slot_id], feat, 1)
            for slot_id in range(slot_count)
        ],
        axis=1,
    )
    lanes = jnp.arange(feat)
    valid = lanes[None, :] < 4 * slot_width[:, None]
    raw_bins = jnp.where(valid[None], spec_tiles.astype(jnp.float32), 0.0)
    counted = jnp.maximum(4 * slot_width, 1).astype(jnp.float32)
    square_mean = jnp.sum(raw_bins * raw_bins, axis=-1, keepdims=True) / counted[None, :, None]
    band_normed = (raw_bins * lax.rsqrt(square_mean + EPSILON)).astype(jnp.bfloat16)
    embedded = jnp.einsum(
        "fsa,asd->fsd", band_normed, w_embed, preferred_element_type=jnp.float32
    ).astype(jnp.bfloat16)
    shards = lax.all_to_all(embedded, BAND, split_axis=0, concat_axis=1, tiled=True)
    selector = holder.astype(jnp.bfloat16)
    packed_tokens = jnp.einsum(
        "fjd,jb->fbd", shards, selector, preferred_element_type=jnp.float32
    ).astype(jnp.bfloat16)
    mixed_tokens, saved = attention_forward(
        packed_tokens, jnp.ones((band_count,), bool), w_qkv, w_proj
    )
    mixed_shards = jnp.einsum(
        "fbd,jb->fjd", mixed_tokens, selector, preferred_element_type=jnp.float32
    ).astype(jnp.bfloat16)
    mixed = lax.all_to_all(mixed_shards, BAND, split_axis=1, concat_axis=0, tiled=True)
    mixed32 = mixed.astype(jnp.float32)
    mixed_normed32, mixed_inv = row_norm(mixed32)
    mixed_normed = mixed_normed32.astype(jnp.bfloat16)
    pre_act = jnp.einsum("fsd,dsh->fsh", mixed_normed, w_hidden, preferred_element_type=jnp.float32)
    tanh_act = jnp.tanh(pre_act)
    hidden_act = tanh_act.astype(jnp.bfloat16)
    output = jnp.einsum("fsh,hse->fse", hidden_act, w_out, preferred_element_type=jnp.float32)
    value_part = output[..., :feat]
    gate_part = jax.nn.sigmoid(output[..., feat:])
    mask_tiles = jnp.where(valid[None], value_part * gate_part, 0.0)
    assembled = jnp.zeros((frame_count, bins_total + feat), jnp.float32)
    for slot_id in range(slot_count):
        offset = 4 * slot_start[slot_id]
        current = lax.dynamic_slice_in_dim(assembled, offset, feat, 1)
        assembled = lax.dynamic_update_slice_in_dim(
            assembled, current + mask_tiles[:, slot_id], offset, 1
        )
    mask = (
        summed_rows(assembled[:, :bins_total].astype(jnp.bfloat16), BAND, 1)
        .astype(jnp.float32)
        .astype(jnp.bfloat16)
    )
    grad_mask = jnp.where(valid[None], cot_tiles.astype(jnp.float32), 0.0)
    grad_value = grad_mask * gate_part
    grad_gate = grad_mask * value_part * gate_part * (1.0 - gate_part)
    grad_output = jnp.concatenate([grad_value, grad_gate], axis=-1).astype(jnp.bfloat16)
    grad_act = jnp.einsum("fse,hse->fsh", grad_output, w_out, preferred_element_type=jnp.float32)
    grad_pre = (grad_act * (1.0 - tanh_act * tanh_act)).astype(jnp.bfloat16)
    grad_normed = jnp.einsum("fsh,dsh->fsd", grad_pre, w_hidden, preferred_element_type=jnp.float32)
    grad_mixed = mixed_inv * (
        grad_normed
        - mixed_normed32 * jnp.mean(grad_normed * mixed_normed32, axis=-1, keepdims=True)
    )
    grad_mixed = grad_mixed.astype(jnp.bfloat16)
    grad_shards = lax.all_to_all(grad_mixed, BAND, split_axis=0, concat_axis=1, tiled=True)
    grad_out = weight_grad(hidden_act, grad_output)
    grad_hidden = weight_grad(mixed_normed, grad_pre)
    grad_packed_tokens = jnp.einsum(
        "fjd,jb->fbd", grad_shards, selector, preferred_element_type=jnp.float32
    ).astype(jnp.bfloat16)
    grad_tokens, grad_qkv, grad_proj = attention_backward(saved, grad_packed_tokens, w_qkv, w_proj)
    grad_tokens = jnp.einsum(
        "fbd,jb->fjd", grad_tokens, selector, preferred_element_type=jnp.float32
    ).astype(jnp.bfloat16)
    grad_qkv, grad_proj = packed_total((grad_qkv, grad_proj), BAND_TM)
    grad_embedded = lax.all_to_all(grad_tokens, BAND, split_axis=1, concat_axis=0, tiled=True)
    grad_embed = weight_grad(band_normed, grad_embedded)
    return (
        mask,
        grad_embed.astype(jnp.bfloat16),
        grad_qkv,
        grad_proj,
        grad_hidden.astype(jnp.bfloat16),
        grad_out.astype(jnp.bfloat16),
    )


def solution(mesh):
    split = Mesh(mesh.devices.reshape(4, 4, mesh.shape["tm"]), ("band_0", "band_1", "tm"))
    placed = (
        P("tm", BAND),
        P("tm", BAND),
        P(),
        P(),
        P(None, BAND, None),
        P(),
        P(),
        P(None, BAND, None),
        P(None, BAND, None),
    )
    return jax.shard_map(
        per_device,
        mesh=split,
        in_specs=placed,
        out_specs=(
            P("tm", BAND),
            P("tm", BAND, None),
            P(),
            P(),
            P("tm", BAND, None),
            P("tm", BAND, None),
        ),
        check_vma=False,
    )
```

profile of v0, /device:TPU:0, one launch (start us, length us, event | category | flops | bytes accessed | tf_op | source)
XLA Modules:
  0.0 512.8 jit_solution(5998383583869793363)
XLA Ops:
  16.3 53.6 %all-gather.2.cloned.1.call-done = bf16[512,4096]{1,0:T(8,128)(2,1)} async-done(((bf16[512,256]{1,0:T(8,128)(2,1)}), bf16[512,4096]{1,0:T(8,128)(2,1)}) %all-gather.2.cloned.1.call-update) | async-done | bytes 4194320 | tf_op jit(solution)/shard_map/all_gather | solution.py:30
  69.9 2.7 fusion.126
  76.9 4.9 all-to-all-start
  81.9 12.9 %all-to-all-done = bf16[256,4,384]{2,1,0:T(4,128)(2,1)S(1)} async-done(((bf16[256,4,384]{2,1,0:T(4,128)(2,1)}), bf16[256,4,384]{2,1,0:T(4,128)(2,1)S(1)}, u32[]{:S(2)}, u32[]{:S(2)}) %all-to-all-start) | async-done | bytes 786464 | tf_op jit(solution)/shard_map/all_to_all | solution.py:206
  100.7 4.3 fusion.129
  104.9 2.2 fusion.39
  108.2 1.8 fusion.48
  110.5 16.2 %all_to_all.78 = bf16[16,64,384]{2,0,1:T(8,128)(2,1)S(1)} all-to-all(bf16[16,64,384]{2,0,1:T(8,128)(2,1)S(1)} %copy.148), channel_id=1, replica_groups=mesh['band_0'=4,'band_1'=4,'tm'=8] {'band_0','band_1'}, dimensions={1} | all-to-all | bytes 1572864 | tf_op jit(solution)/shard_map/all_to_all | solution.py:217
  127.6 4.7 fusion.8
  132.4 2.3 fusion.20
  136.4 6.0 %fusion.12 = bf16[256,4,1536]{2,0,1:T(8,128)(2,1)} fusion(f32[4,256,1536]{2,1,0:T(8,128)S(1)} %fusion.8, bf16[1536,4,512]{2,1,0:T(4,128)(2,1)S(1)} %bitcast.157, bf16[256,4,256]{2,0,1:T(8,128)(2,1)} %get-tuple-element.23, bf16[256,4,256]{2,0,1:T(8,128)(2,1)S(1)} %get-tuple-element.22), kind=kOutput, calls=%fused_computation.15 | convolution fusion | flops 1619001344 | bytes 16777216 | tf_op jit(solution)/shard_map/fse,hse->fsh/dot_general | solution.py:244
  142.4 5.3 %fusion.23 = (f32[256,4]{0,1:T(4,128)S(1)}, f32[4,256,384]{2,1,0:T(8,128)S(1)}) fusion(f32[16,16,4,384]{3,0,1,2:T(8,128)S(1)} %copy.149, f32[256,4]{0,1:T(4,128)S(1)} %rsqrt.30, bf16[256,4,1536]{2,0,1:T(8,128)(2,1)} %fusion.12, bf16[384,4,1536]{2,1,0:T(4,128)(2,1)} %param.16), kind=kOutput, calls=%fused_computation.38 | convolution fusion | flops 1209138176 | bytes 11018240 | tf_op jit(solution)/shard_map/fsh,dsh->fsd/dot_general | solution.py:246
  148.8 15.4 %all_to_all.79 = bf16[256,4,384]{2,1,0:T(4,128)(2,1)S(1)} all-to-all(bf16[256,4,384]{2,1,0:T(4,128)(2,1)S(1)} %copy.157), channel_id=1, replica_groups=mesh['band_0'=4,'band_1'=4,'tm'=8] {'band_0','band_1'}, dimensions={0} | all-to-all | bytes 1572864 | tf_op jit(solution)/shard_map/all_to_all | solution.py:252
  167.0 2.3 convolution_convert_fusion.8
  169.3 2.4 reshape.213
  171.7 3.7 fusion.66
  176.8 5.7 %fusion.44 = bf16[16,32,8,64]{3,1,2,0:T(8,128)(2,1)} fusion(f32[16,8,32,32]{2,3,1,0:T(8,128)} %fusion.66, bf16[16,32,8,64]{3,2,1,0:T(8,128)(2,1)} %reshape.211, f32[16,8,32,32]{2,3,1,0:T(8,128)} %get-tuple-element.45, f32[16,8,32]{2,1,0:T(8,128)S(1)} %copy-done.31), kind=kOutput, calls=%fused_computation.56 | convolution fusion | flops 17960992 | bytes 2113536 | tf_op jit(solution)/shard_map/nhqk,nkhc->nqhc/dot_general | solution.py:128
  182.5 5.7 %fusion.41 = bf16[16,32,8,64]{3,1,2,0:T(8,128)(2,1)} fusion(f32[16,8,32,32]{2,3,1,0:T(8,128)} %fusion.66, bf16[16,32,8,64]{3,2,1,0:T(8,128)(2,1)} %reshape.210, f32[16,8,32,32]{2,3,1,0:T(8,128)} %get-tuple-element.45, f32[16,8,32]{2,1,0:T(8,128)S(1)} %copy-done.31), kind=kOutput, calls=%fused_computation.55 | convolution fusion | flops 17960992 | bytes 2113536 | tf_op jit(solution)/shard_map/nhqk,nqhc->nkhc/dot_general | solution.py:131
  188.2 2.6 copy.167
  190.8 2.6 reshape.216
  193.4 2.6 copy.165
  196.0 2.6 reshape.215
  198.6 2.6 copy.163
  201.2 2.6 reshape.214
  208.3 14.8 %all_to_all.80 = bf16[16,64,384]{2,0,1:T(8,128)(2,1)S(1)} all-to-all(bf16[16,64,384]{2,0,1:T(8,128)(2,1)S(1)} %copy.168), channel_id=1, replica_groups=mesh['band_0'=4,'band_1'=4,'tm'=8] {'band_0','band_1'}, dimensions={1} | all-to-all | bytes 1572864 | tf_op jit(solution)/shard_map/all_to_all | solution.py:263
  224.8 4.8 all-to-all-start.4
  229.6 3.3 convolution_convert_fusion
  232.9 2.6 copy.174
  235.5 7.2 %all-to-all-done.4 = bf16[8,32,4,384]{3,1,2,0:T(8,128)(2,1)} async-done(((bf16[8,32,4,384]{3,1,2,0:T(8,128)(2,1)}), bf16[8,32,4,384]{3,1,2,0:T(8,128)(2,1)}, u32[]{:S(2)}, u32[]{:S(2)}) %all-to-all-start.4) | async-done | bytes 786464 | tf_op jit(solution)/shard_map/all_to_all | solution.py:23
  242.7 4.6 all-to-all-start.5
  247.4 2.4 broadcast_in_dim.82
  249.9 2.1 dynamic_update_slice.12
  253.1 1.8 dynamic_update_slice.13
  256.1 1.8 dynamic_update_slice.14
  259.0 1.8 dynamic_update_slice.15
  260.9 3.9 slice.133
  266.0 7.3 %convert_bitcast_fusion = bf16[1536,4,512]{0,2,1:T(8,128)(2,1)} fusion(f32[4,256,1536]{2,1,0:T(8,128)} %copy-done.2, bf16[256,4,256]{2,0,1:T(8,128)(2,1)S(1)} %copy-done.12, bf16[256,4,256]{2,0,1:T(8,128)(2,1)S(1)} %copy-done.11), kind=kOutput, calls=%fused_computation.2 | convolution fusion | flops 1617428480 | bytes 13631488 | tf_op jit(solution)/shard_map/fsa,fsb->asb/dot_general | solution.py:152
  273.3 8.6 %copy.177 = bf16[1536,4,512]{2,0,1:T(8,128)(2,1)} copy(bf16[1536,4,512]{0,2,1:T(8,128)(2,1)} %convert_bitcast_fusion) | data formatting | bytes 12582912 | tf_op jit(solution)/shard_map/convert_element_type | solution.py:152
  281.9 6.2 %copy.178 = bf16[8,192,4,512]{3,1,2,0:T(8,128)(2,1)} copy(bf16[8,192,4,512]{3,1,0,2:T(8,128)(2,1)} %bitcast.154) | data formatting | bytes 12582912 | tf_op jit(solution)/shard_map/reshape | solution.py:17
  290.7 3.7 convolution_bitcast_fusion
  294.4 2.3 reshape.218
  296.7 5.9 %all-to-all-done.5 = bf16[8,48,4,1536]{3,1,2,0:T(8,128)(2,1)} async-done(((bf16[8,48,4,1536]{3,1,2,0:T(8,128)(2,1)}), bf16[8,48,4,1536]{3,1,2,0:T(8,128)(2,1)}, u32[]{:S(2)}, u32[]{:S(2)}) %all-to-all-start.5) | async-done | bytes 4718624 | tf_op jit(solution)/shard_map/all_to_all | solution.py:23
  302.6 4.8 all-to-all-start.6
  307.4 1.9 pad_maximum_fusion
  311.8 171.5 %all-reduce.4.cloned.1.call-done = f32[786432]{0:T(1024)} async-done(((f32[786432]{0:T(1024)}), f32[786432]{0:T(1024)}) %all-reduce.4.cloned.1.call-update) | async-done | bytes 3145744 | tf_op jit(solution)/shard_map/psum | solution.py:44
  487.6 3.1 reduce_sum.140
  491.9 4.0 reduce_sum.141
  497.4 8.4 %reduce-scatter.5.cloned.1.call-done = bf16[256,256]{1,0:T(8,128)(2,1)} async-done(((bf16[256,1024]{1,0:T(8,128)(2,1)}), bf16[256,256]{1,0:T(8,128)(2,1)}) %reduce-scatter.5.cloned.1.call-update) | async-done | bytes 131088 | tf_op jit(solution)/shard_map/reduce_scatter | solution.py:36
  (150 shorter events, 48.8 us)
Async XLA Ops:
  7.2 88.6 %copy-start = (bf16[384,1536]{1,0:T(8,128)(2,1)S(1)}, bf16[384,1536]{1,0:T(8,128)(2,1)}, u32[]{:S(2)}) copy-start(bf16[384,1536]{1,0:T(8,128)(2,1)} %param.14) | copy-start | bytes 3538948
  7.2 62.7 %all-gather.2.cloned.1.call-start = ((), (), s32[]{:S(2)}) async-start(), calls=%async_computation.9 | async-start | bytes 4456448 | tf_op jit(solution)/shard_map/all_gather | solution.py:30
  72.6 2.3 copy-start.27
  74.0 1.4 copy-start.17
  74.0 1.4 copy-start.19
  74.0 1.4 copy-start.21
  74.0 1.4 copy-start.23
  74.3 0.6 copy-start.25
  75.4 6.5 %copy-start.28 = (s32[32]{0:T(128)S(1)}, s32[32]{0:T(128)}, u32[]{:S(2)}) copy-start(s32[32]{0:T(128)} %param.12) | copy-start | bytes 388
  76.9 17.9 %all-to-all-start = ((bf16[256,4,384]{2,1,0:T(4,128)(2,1)}), bf16[256,4,384]{2,1,0:T(4,128)(2,1)S(1)}, u32[]{:S(2)}, u32[]{:S(2)}) async-start(bf16[256,4,384]{2,1,0:T(4,128)(2,1)} %copy.141), calls=%async_computation | async-start | bytes 1572864 | tf_op jit(solution)/shard_map/all_to_all | solution.py:206
  100.7 4.3 copy-start.4
  104.9 2.2 copy-start.30
  108.2 18.5 %copy-start.8 = (bf16[16,32,512]{2,1,0:T(8,128)(2,1)}, bf16[16,32,512]{2,1,0:T(8,128)(2,1)S(1)}, u32[]{:S(2)}) copy-start(bf16[16,32,512]{2,1,0:T(8,128)(2,1)S(1)} %reshape.212) | copy-start | bytes 1572868
  127.3 5.0 slice-start
  127.6 4.8 slice-start.1
  132.3 4.1 copy-start.2
  132.3 2.4 copy-start.13
  132.3 2.4 copy-start.14
  132.4 2.4 copy-start.15
  132.4 2.4 copy-start.16
  136.4 6.0 %copy-start.10 = (bf16[256,4,256]{2,0,1:T(8,128)(2,1)}, bf16[256,4,256]{2,0,1:T(8,128)(2,1)S(1)}, u32[]{:S(2)}) copy-start(bf16[256,4,256]{2,0,1:T(8,128)(2,1)S(1)} %get-tuple-element.22) | copy-start | bytes 1572868
  171.7 3.7 copy-start.5
  171.7 3.7 copy-start.29
  171.7 3.7 copy-start.31
  203.8 2.2 copy-start.7
  206.1 1.1 copy-start.6
  207.7 15.4 %copy-start.18 = (bf16[256,1,256]{2,0,1:T(8,128)(2,1)S(1)}, bf16[256,1,256]{2,0,1:T(8,128)(2,1)}, u32[]{:S(2)}) copy-start(bf16[256,1,256]{2,0,1:T(8,128)(2,1)} %copy-done.17) | copy-start | bytes 393220
  207.7 15.4 %copy-start.20 = (bf16[256,1,256]{2,0,1:T(8,128)(2,1)S(1)}, bf16[256,1,256]{2,0,1:T(8,128)(2,1)}, u32[]{:S(2)}) copy-start(bf16[256,1,256]{2,0,1:T(8,128)(2,1)} %copy-done.19) | copy-start | bytes 393220
  207.8 15.4 %copy-start.22 = (bf16[256,1,256]{2,0,1:T(8,128)(2,1)S(1)}, bf16[256,1,256]{2,0,1:T(8,128)(2,1)}, u32[]{:S(2)}) copy-start(bf16[256,1,256]{2,0,1:T(8,128)(2,1)} %copy-done.21) | copy-start | bytes 393220
  207.8 15.4 %copy-start.24 = (bf16[256,1,256]{2,0,1:T(8,128)(2,1)S(1)}, bf16[256,1,256]{2,0,1:T(8,128)(2,1)}, u32[]{:S(2)}) copy-start(bf16[256,1,256]{2,0,1:T(8,128)(2,1)} %copy-done.23) | copy-start | bytes 393220
  207.8 15.4 %copy-start.26 = (f32[256,4]{0,1:T(4,128)S(1)}, f32[256,4]{0,1:T(4,128)}, u32[]{:S(2)}) copy-start(f32[256,4]{0,1:T(4,128)} %copy-done.25) | copy-start | bytes 12292
  224.8 17.9 %all-to-all-start.4 = ((bf16[8,32,4,384]{3,1,2,0:T(8,128)(2,1)}), bf16[8,32,4,384]{3,1,2,0:T(8,128)(2,1)}, u32[]{:S(2)}, u32[]{:S(2)}) async-start(bf16[8,32,4,384]{3,1,2,0:T(8,128)(2,1)} %copy.171), calls=%async_computation.6 | async-start | bytes 1572864 | tf_op jit(solution)/shard_map/all_to_all | solution.py:23
  235.5 11.9 %copy-start.3 = (f32[256,4,256]{2,0,1:T(8,128)S(1)}, f32[256,4,256]{2,0,1:T(8,128)}, u32[]{:S(2)}) copy-start(f32[256,4,256]{2,0,1:T(8,128)} %get-tuple-element.24) | copy-start | bytes 3145732
  242.7 59.9 %all-to-all-start.5 = ((bf16[8,48,4,1536]{3,1,2,0:T(8,128)(2,1)}), bf16[8,48,4,1536]{3,1,2,0:T(8,128)(2,1)}, u32[]{:S(2)}, u32[]{:S(2)}) async-start(bf16[8,48,4,1536]{3,1,2,0:T(8,128)(2,1)} %copy.174), calls=%async_computation.7 | async-start | bytes 9437184 | tf_op jit(solution)/shard_map/all_to_all | solution.py:23
  247.3 62.0 %reduce-scatter.3.cloned.1.call-start = ((), (), s32[]{:S(2)}) async-start(), calls=%async_computation.10 | async-start | bytes 2621440 | tf_op jit(solution)/shard_map/reduce_scatter | solution.py:36
  264.8 1.0 copy-start.11
  264.8 1.2 copy-start.12
  281.9 6.2 %copy-start.9 = (bf16[16,32,512]{2,1,0:T(8,128)(2,1)S(1)}, bf16[16,32,512]{2,1,0:T(8,128)(2,1)}, u32[]{:S(2)}) copy-start(bf16[16,32,512]{2,1,0:T(8,128)(2,1)} %copy-done.8) | copy-start | bytes 1572868
  302.6 189.3 %all-to-all-start.6 = ((bf16[8,192,4,512]{3,1,2,0:T(8,128)(2,1)}), bf16[8,192,4,512]{3,1,2,0:T(8,128)(2,1)}, u32[]{:S(2)}, u32[]{:S(2)}) async-start(bf16[8,192,4,512]{3,1,2,0:T(8,128)(2,1)} %copy.178), calls=%async_computation.8 | async-start | bytes 12582912 | tf_op jit(solution)/shard_map/all_to_all | solution.py:23
  307.4 175.9 %all-reduce.4.cloned.1.call-start = ((), (), s32[]{:S(2)}) async-start(), calls=%async_computation.12 | async-start | bytes 6291456 | tf_op jit(solution)/shard_map/psum | solution.py:44
  309.3 196.5 %reduce-scatter.5.cloned.1.call-start = ((), (), s32[]{:S(2)}) async-start(), calls=%async_computation.11 | async-start | bytes 655360 | tf_op jit(solution)/shard_map/reduce_scatter | solution.py:36
  483.3 1.7 slice-start.2
  484.9 1.6 slice-start.3
  491.9 13.9 %copy-start.1 = (bf16[384,1536]{1,0:T(8,128)(2,1)S(1)}, bf16[384,1536]{1,0:T(8,128)(2,1)}, u32[]{:S(2)}) copy-start(bf16[384,1536]{1,0:T(8,128)(2,1)} %param.14) | copy-start | bytes 3538948
Sparse Core Ops, SparseCore 0:
  10.7 59.1 all-gather.1
  264.9 27.9 reduce-scatter.2
  312.9 170.3 all-reduce.3
  486.1 19.6 reduce-scatter.4
where the time goes:
time: 522 us; the launch traced here: 513 us
  waiting for transfers between devices  260 us (50%)
  local copies, waits for them, and re-layouts  81.6 us (16%)
  matrix products  66.6 us (13%)
  blocking collectives  46.4 us (9%)
  other arithmetic  21.4 us (4%)
  starting transfers between devices  19.2 us (4%)
  between operations  17.5 us (3%)
    psum x1, waiting for transfers between devices, packed_total(): subtotal = lax.psum(jnp.concatenate([a.ravel() for a in arrays]), axis)  171 us
    all_gather x1, waiting for transfers between devices, in_one_piece(): out = lax.all_gather(both, axis, axis=dim, tiled=True)  53.6 us
    all_to_all x1, blocking collectives, per_device(): lax.all_to_all(mixed_shards, BAND, split_axis=1, concat_axis=0, tiled=True)  16.2 us
    all_to_all x1, blocking collectives, per_device(): lax.all_to_all(grad_mixed, BAND, split_axis=0, concat_axis=1, tiled=True)  15.4 us
    all_to_all x1, blocking collectives, per_device(): lax.all_to_all(grad_tokens, BAND, split_axis=1, concat_axis=0, tiled=True)  14.8 us
    all_to_all x3, starting transfers between devices, sent_and_summed(): lax.all_to_all(cut_along(shard, dim, peers), axis, 0, 0, tiled=True)  14.1 us
    all_to_all x3, waiting for transfers between devices, sent_and_summed(): lax.all_to_all(cut_along(shard, dim, peers), axis, 0, 0, tiled=True)  13.1 us
    all_to_all x1, waiting for transfers between devices, per_device(): lax.all_to_all(embedded, BAND, split_axis=0, concat_axis=1, tiled=True)  12.9 us
  transfers between devices with their start and end apart: 8, of which 6 were waited for; matrix products, arithmetic and copies ran while one was open for 15% of the time, Pallas kernels for 0%

commit v1 on v0

v1 whole, which is shorter than its diff:
```python
import functools

import jax
import jax.numpy as jnp
from jax import lax
from jax.experimental import pallas as pl
from jax.experimental.pallas import tpu as pltpu
from jax.sharding import Mesh
from jax.sharding import PartitionSpec as P

HEAD_DIM = 64
EPSILON = 1e-05
MESH = pl.DeviceIdType.MESH
BF16 = jnp.bfloat16
F32 = jnp.float32
VMEM = pl.BlockSpec(memory_space=pltpu.VMEM)
SMEM = pl.BlockSpec(memory_space=pltpu.SMEM)
LIMIT = 60 * 1024 * 1024


def dot(a, b, da, db):
    return lax.dot_general(a, b, (((da,), (db,)), ((), ())), preferred_element_type=F32)


def plain(body, outs, ins, scratch=(), flops=1_000_000_000, out_specs=None):
    return pl.pallas_call(
        body,
        out_shape=outs,
        in_specs=ins,
        out_specs=out_specs if out_specs is not None else [VMEM] * len(outs),
        scratch_shapes=scratch,
        compiler_params=pltpu.CompilerParams(vmem_limit_bytes=LIMIT),
        cost_estimate=pl.CostEstimate(flops=flops, bytes_accessed=4_000_000, transcendentals=0),
    )


def place(nx, ny, index, cores):
    if cores == 2:
        chip = index // 2
        return {"x": chip // ny, "y": chip % ny, "c": index % 2}
    return {"x": index // ny, "y": index % ny}


def exchange_body(nx, ny, cores, count, *refs):
    ins, outs, (send, recv, local) = refs[:count], refs[count : 2 * count], refs[2 * count :]
    me = lax.axis_index("x") * ny + lax.axis_index("y")
    if cores == 2:
        me = me * 2 + lax.axis_index("c")
    peers = nx * ny * cores
    barrier = pltpu.get_barrier_semaphore()
    for k in range(1, peers):
        peer = lax.rem(me + k, peers)
        pl.semaphore_signal(barrier, inc=1, device_id=place(nx, ny, peer, cores), device_id_type=MESH)
    own = []
    for a in range(count):
        own.append(pltpu.make_async_copy(ins[a].at[me], outs[a].at[me], local.at[a]))
        own[-1].start()
    pl.semaphore_wait(barrier, peers - 1)
    copies = []
    for a in range(count):
        for k in range(1, peers):
            peer = lax.rem(me + k, peers)
            copies.append(
                pltpu.make_async_remote_copy(
                    src_ref=ins[a].at[peer],
                    dst_ref=outs[a].at[me],
                    send_sem=send.at[a, k],
                    recv_sem=recv.at[a, k],
                    device_id=place(nx, ny, peer, cores),
                    device_id_type=MESH,
                )
            )
            copies[-1].start()
    for copy in own:
        copy.wait()
    for copy in copies:
        copy.wait()


def exchange(arrays, sizes, cores, ident):
    nx, ny = sizes
    peers = nx * ny * cores
    count = len(arrays)
    return pl.pallas_call(
        functools.partial(exchange_body, nx, ny, cores, count),
        out_shape=[jax.ShapeDtypeStruct(a.shape, a.dtype) for a in arrays],
        in_specs=[VMEM] * count,
        out_specs=[VMEM] * count,
        scratch_shapes=[
            pltpu.SemaphoreType.DMA((count, peers)),
            pltpu.SemaphoreType.DMA((count, peers)),
            pltpu.SemaphoreType.DMA((count,)),
        ],
        compiler_params=pltpu.CompilerParams(
            collective_id=ident, has_side_effects=True, vmem_limit_bytes=16 * 1024 * 1024
        ),
        cost_estimate=pl.CostEstimate(flops=1_000_000_000, bytes_accessed=4_000_000, transcendentals=0),
    )(*arrays)


def tiles_body(spec_ref, cot_ref, widths_ref, group_ref, normed_ref, cots_ref, starts_ref, slots_ref, full, counts):
    parts, frames, cols = spec_ref.shape
    groups = counts.shape[0]
    slot_count = normed_ref.shape[0] // groups
    feat = normed_ref.shape[2]
    bands = widths_ref.shape[0]
    for p in range(parts):
        full[0, :, p * cols : (p + 1) * cols] = spec_ref[p].astype(F32)
        full[1, :, p * cols : (p + 1) * cols] = cot_ref[p].astype(F32)
    total = parts * cols
    full[:, :, total:] = jnp.zeros((2, frames, full.shape[2] - total), F32)
    normed_ref[...] = jnp.zeros_like(normed_ref)
    cots_ref[...] = jnp.zeros_like(cots_ref)
    for g in range(groups):
        counts[g] = 0
    window = feat + 128
    lane = lax.broadcasted_iota(jnp.int32, (frames, feat), 1)

    def step(b, start):
        width = widths_ref[b]
        group = group_ref[b]
        rank = counts[group]
        counts[group] = rank + 1
        slot = group * slot_count + rank
        starts_ref[b] = start
        slots_ref[b] = slot
        offset = 4 * start
        base = pl.multiple_of((offset // 128) * 128, 128)
        shift = lax.rem(window - (offset - base), window)
        raw = pltpu.roll(full[0, :, pl.ds(base, window)], shift, 1)[:, :feat]
        cot = pltpu.roll(full[1, :, pl.ds(base, window)], shift, 1)[:, :feat]
        valid = lane < 4 * width
        raw = jnp.where(valid, raw, 0.0)
        cot = jnp.where(valid, cot, 0.0)
        counted = jnp.full((frames, 1), 4 * width, jnp.int32).astype(F32)
        mean = jnp.sum(raw * raw, axis=1, keepdims=True) / counted
        normed_ref[slot] = (raw * lax.rsqrt(mean + EPSILON)).astype(BF16)
        cots_ref[slot] = cot.astype(BF16)
        return start + width

    lax.fori_loop(0, bands, step, jnp.int32(0))


def band_tiles(spec_rows, cot_rows, widths, band_group, groups, slot_count, feat):
    parts, frames, cols = spec_rows.shape
    bands = widths.shape[0]
    tile = jax.ShapeDtypeStruct((groups * slot_count, frames, feat), BF16)
    ints = jax.ShapeDtypeStruct((bands,), jnp.int32)
    return plain(
        tiles_body,
        [tile, tile, ints, ints],
        [VMEM, VMEM, SMEM, SMEM],
        [pltpu.VMEM((2, frames, parts * cols + feat + 128), F32), pltpu.SMEM((groups,), jnp.int32)],
        out_specs=[VMEM, VMEM, SMEM, SMEM],
    )(spec_rows, cot_rows, widths, band_group)


def mask_body(tile_ref, widths_ref, starts_ref, slots_ref, out_ref, full):
    parts, frames, cols = out_ref.shape
    feat = tile_ref.shape[2]
    window = feat + 128
    full[...] = jnp.zeros_like(full)
    lane = lax.broadcasted_iota(jnp.int32, (frames, window), 1)

    def step(b, carry):
        offset = 4 * starts_ref[b]
        base = pl.multiple_of((offset // 128) * 128, 128)
        tile = tile_ref[slots_ref[b]].astype(F32)
        wide = jnp.concatenate([tile, jnp.zeros((frames, 128), F32)], axis=1)
        wide = jnp.where(lane < 4 * widths_ref[b], wide, 0.0)
        full[:, pl.ds(base, window)] += pltpu.roll(wide, offset - base, 1)
        return carry

    lax.fori_loop(0, widths_ref.shape[0], step, 0)
    for p in range(parts):
        out_ref[p] = full[:, p * cols : (p + 1) * cols].astype(BF16)


def mask_rows(tiles, widths, starts, slots, parts, cols):
    frames = tiles.shape[1]
    return plain(
        mask_body,
        [jax.ShapeDtypeStruct((parts, frames, cols), BF16)],
        [VMEM, SMEM, SMEM, SMEM],
        [pltpu.VMEM((frames, parts * cols + tiles.shape[2] + 128), F32)],
    )(tiles, widths, starts, slots)[0]


def embed_body(normed_ref, w_ref, out_ref):
    peers, slots, frames, feat = normed_ref.shape
    for s in range(slots):
        rows = normed_ref[:, s].reshape(peers * frames, feat)
        out_ref[:, s] = dot(rows, w_ref[s], 1, 0).astype(BF16).reshape(peers, frames, -1)


def embed(normed, w):
    peers, slots, frames, _ = normed.shape
    return plain(
        embed_body, [jax.ShapeDtypeStruct((peers, slots, frames, w.shape[2]), BF16)], [VMEM, VMEM]
    )(normed, w)[0]


def embed_grad_body(normed_ref, grad_ref, out_ref):
    peers, slots, frames, feat = normed_ref.shape
    for s in range(slots):
        rows = normed_ref[:, s].reshape(peers * frames, feat)
        grads = grad_ref[:, s].reshape(peers * frames, grad_ref.shape[3])
        out_ref[s] = dot(rows, grads, 0, 0).astype(BF16)


def embed_grad(normed, grads):
    _, slots, _, feat = normed.shape
    return plain(
        embed_grad_body,
        [jax.ShapeDtypeStruct((slots, feat, grads.shape[3]), BF16)],
        [VMEM, VMEM],
    )(normed, grads)[0]


def to_frames(rows, frames, bands):
    out = lax.broadcasted_iota(jnp.int32, (rows, rows), 0)
    src = lax.broadcasted_iota(jnp.int32, (rows, rows), 1)
    return ((out // bands == src % frames) & (out % bands == src // frames)).astype(F32).astype(BF16)


def to_bands(rows, frames, bands):
    out = lax.broadcasted_iota(jnp.int32, (rows, rows), 0)
    src = lax.broadcasted_iota(jnp.int32, (rows, rows), 1)
    return ((src // bands == out % frames) & (src % bands == out // frames)).astype(F32).astype(BF16)


BLOCK = 128


def forward_body(tok_ref, slots_ref, w_qkv_ref, w_proj_ref, mixed_ref, rows_ref, packed_ref, soft_ref, heads_ref, stage):
    _, frames, width = tok_ref.shape
    bands = slots_ref.shape[0]
    rows = bands * frames
    inner = w_proj_ref.shape[0]
    heads = inner // HEAD_DIM
    for b in range(bands):
        stage[b] = tok_ref[slots_ref[b]]
    tokens32 = dot(to_frames(rows, frames, bands), stage[...].reshape(rows, width), 1, 0)
    rows_ref[...] = tokens32.astype(BF16)
    inv = lax.rsqrt(jnp.mean(tokens32 * tokens32, axis=1, keepdims=True) + EPSILON)
    normed = (tokens32 * inv).astype(BF16)
    packed_ref[...] = dot(normed, w_qkv_ref[...], 1, 0).astype(BF16)
    row_id = lax.broadcasted_iota(jnp.int32, (BLOCK, BLOCK), 0) // bands
    col_id = lax.broadcasted_iota(jnp.int32, (BLOCK, BLOCK), 1) // bands
    same = row_id == col_id

    def step(i, carry):
        at = pl.ds(pl.multiple_of(i * BLOCK, BLOCK), BLOCK)
        outs = []
        for h in range(heads):
            lo = h * HEAD_DIM
            q = packed_ref[at, lo : lo + HEAD_DIM]
            k = packed_ref[at, inner + lo : inner + lo + HEAD_DIM]
            v = packed_ref[at, 2 * inner + lo : 2 * inner + lo + HEAD_DIM]
            scores = jnp.where(same, dot(q, k, 1, 1) * HEAD_DIM ** (-0.5), -jnp.inf)
            expd = jnp.exp(scores - jnp.max(scores, axis=1, keepdims=True))
            soft = expd / jnp.sum(expd, axis=1, keepdims=True)
            soft_ref[h, at, :] = soft
            outs.append(dot(soft.astype(BF16), v, 1, 0))
        heads_ref[at, :] = jnp.concatenate(outs, axis=1).astype(BF16)
        return carry

    lax.fori_loop(0, rows // BLOCK, step, 0)
    mixed = (tokens32 + dot(heads_ref[...], w_proj_ref[...], 1, 0)).astype(BF16)
    stage[...] = dot(to_bands(rows, frames, bands), mixed, 1, 0).astype(BF16).reshape(bands, frames, width)
    mixed_ref[...] = jnp.zeros_like(mixed_ref)
    for b in range(bands):
        mixed_ref[slots_ref[b]] = stage[b]


def attention_forward(tokens, slots, w_qkv, w_proj):
    _, frames, width = tokens.shape
    bands = slots.shape[0]
    rows = bands * frames
    inner = w_proj.shape[0]
    return plain(
        forward_body,
        [
            jax.ShapeDtypeStruct(tokens.shape, BF16),
            jax.ShapeDtypeStruct((rows, width), BF16),
            jax.ShapeDtypeStruct((rows, 3 * inner), BF16),
            jax.ShapeDtypeStruct((inner // HEAD_DIM, rows, BLOCK), F32),
            jax.ShapeDtypeStruct((rows, inner), BF16),
        ],
        [VMEM, SMEM, VMEM, VMEM],
        [pltpu.VMEM((bands, frames, width), BF16)],
    )(tokens, slots, w_qkv, w_proj)


def backward_body(
    grad_ref, slots_ref, w_qkv_ref, w_proj_ref, rows_ref, packed_ref, soft_ref, heads_ref,
    out_ref, sums_ref, stage, dheads, dpacked,
):
    _, frames, width = grad_ref.shape
    bands = slots_ref.shape[0]
    rows = bands * frames
    inner = w_proj_ref.shape[0]
    heads = inner // HEAD_DIM
    for b in range(bands):
        stage[b] = grad_ref[slots_ref[b]]
    grad32 = dot(to_frames(rows, frames, bands), stage[...].reshape(rows, width), 1, 0)
    grads = grad32.astype(BF16)
    dheads[...] = dot(grads, w_proj_ref[...], 1, 1).astype(BF16)

    def step(i, carry):
        at = pl.ds(pl.multiple_of(i * BLOCK, BLOCK), BLOCK)
        dq, dk, dv = [], [], []
        for h in range(heads):
            lo = h * HEAD_DIM
            q = packed_ref[at, lo : lo + HEAD_DIM]
            k = packed_ref[at, inner + lo : inner + lo + HEAD_DIM]
            v = packed_ref[at, 2 * inner + lo : 2 * inner + lo + HEAD_DIM]
            g = dheads[at, lo : lo + HEAD_DIM]
            soft = soft_ref[h, at, :]
            p_grad = dot(g, v, 1, 1)
            dv.append(dot(soft.astype(BF16), g, 0, 0))
            spread = soft * (p_grad - jnp.sum(p_grad * soft, axis=1, keepdims=True))
            spread = (spread * HEAD_DIM ** (-0.5)).astype(BF16)
            dq.append(dot(spread, k, 1, 0))
            dk.append(dot(spread, q, 0, 0))
        dpacked[at, :] = jnp.concatenate(dq + dk + dv, axis=1).astype(BF16)
        return carry

    lax.fori_loop(0, rows // BLOCK, step, 0)
    tokens32 = rows_ref[...].astype(F32)
    inv = lax.rsqrt(jnp.mean(tokens32 * tokens32, axis=1, keepdims=True) + EPSILON)
    normed32 = tokens32 * inv
    gn = dot(dpacked[...], w_qkv_ref[...], 1, 1)
    back = grad32 + inv * (gn - normed32 * jnp.mean(gn * normed32, axis=1, keepdims=True))
    stage[...] = (
        dot(to_bands(rows, frames, bands), back.astype(BF16), 1, 0).astype(BF16).reshape(bands, frames, width)
    )
    out_ref[...] = jnp.zeros_like(out_ref)
    for b in range(bands):
        out_ref[slots_ref[b]] = stage[b]
    pieces, depth, _ = sums_ref.shape
    small = inner // pieces
    tall = depth - small
    across = 3 * inner // width
    proj = dot(heads_ref[...], grads, 0, 0).astype(BF16)
    sums_ref[:, tall:, :] = proj.reshape(pieces, small, width)
    normed = normed32.astype(BF16)
    for j in range(across):
        part = dot(normed, dpacked[:, j * width : (j + 1) * width], 0, 0).astype(BF16)
        for i in range(pieces // across):
            sums_ref[i * across + j, :tall, :] = part[i * tall : (i + 1) * tall, :]


def attention_backward(grads, slots, w_qkv, w_proj, saved, pieces):
    _, frames, width = grads.shape
    bands = slots.shape[0]
    rows = bands * frames
    inner = w_proj.shape[0]
    depth = (3 * inner * width + inner * width) // pieces // width
    return plain(
        backward_body,
        [
            jax.ShapeDtypeStruct(grads.shape, BF16),
            jax.ShapeDtypeStruct((pieces, depth, width), BF16),
        ],
        [VMEM, SMEM] + [VMEM] * 6,
        [
            pltpu.VMEM((bands, frames, width), BF16),
            pltpu.VMEM((rows, inner), BF16),
            pltpu.VMEM((rows, 3 * inner), BF16),
        ],
    )(grads, slots, w_qkv, w_proj, *saved)


def unpack_body(sums_ref, qkv_ref, proj_ref):
    pieces, depth, width = sums_ref.shape
    small = proj_ref.shape[0] // pieces
    tall = depth - small
    across = qkv_ref.shape[1] // width
    proj_ref[...] = sums_ref[:, tall:, :].astype(F32).reshape(proj_ref.shape)
    for i in range(pieces // across):
        for j in range(across):
            qkv_ref[i * tall : (i + 1) * tall, j * width : (j + 1) * width] = sums_ref[
                i * across + j, :tall, :
            ].astype(F32)


def tail_body(mixed_ref, cot_ref, wh_ref, wo_ref, mask_ref, dmix_ref, gh_ref, go_ref, normed, hidden, dout, dpre):
    peers, _, frames, width = mixed_ref.shape
    feat = cot_ref.shape[3]
    rows = peers * frames
    chunk = min(rows, 256)
    lump = chunk // frames

    def step(i, carry):
        at = pl.ds(pl.multiple_of(i * chunk, chunk), chunk)
        who = pl.ds(i * lump, lump)
        x = mixed_ref[who, 0].reshape(chunk, width).astype(F32)
        inv = lax.rsqrt(jnp.mean(x * x, axis=1, keepdims=True) + EPSILON)
        n = x * inv
        nb = n.astype(BF16)
        normed[at, :] = nb
        t = jnp.tanh(dot(nb, wh_ref[0], 1, 0))
        hb = t.astype(BF16)
        hidden[at, :] = hb
        out = dot(hb, wo_ref[0], 1, 0)
        value = out[:, :feat]
        gate = jax.nn.sigmoid(out[:, feat:])
        mask_ref[who, 0] = (value * gate).astype(BF16).reshape(lump, frames, feat)
        c = cot_ref[who, 0].reshape(chunk, feat).astype(F32)
        cg = c * gate
        g = jnp.concatenate([cg, cg * value * (1.0 - gate)], axis=1).astype(BF16)
        dout[at, :] = g
        gp = (dot(g, wo_ref[0], 1, 1) * (1.0 - t * t)).astype(BF16)
        dpre[at, :] = gp
        gn = dot(gp, wh_ref[0], 1, 1)
        dm = inv * (gn - n * jnp.mean(gn * n, axis=1, keepdims=True))
        dmix_ref[who, 0] = dm.astype(BF16).reshape(lump, frames, width)
        return carry

    lax.fori_loop(0, rows // chunk, step, 0)
    go_ref[0] = dot(hidden[...], dout[...], 0, 0).astype(BF16)
    gh_ref[0] = dot(normed[...], dpre[...], 0, 0).astype(BF16)


def tail(mixed, cots, w_hidden, w_out):
    peers, slots, frames, width = mixed.shape
    feat = cots.shape[3]
    hid = w_hidden.shape[2]
    rows = peers * frames

    def tile(last):
        return pl.BlockSpec((peers, 1, frames, last), lambda s: (0, s, 0, 0))

    def weight(a, b):
        return pl.BlockSpec((1, a, b), lambda s: (s, 0, 0))

    return pl.pallas_call(
        tail_body,
        grid=(slots,),
        out_shape=[
            jax.ShapeDtypeStruct((peers, slots, frames, feat), BF16),
            jax.ShapeDtypeStruct((peers, slots, frames, width), BF16),
            jax.ShapeDtypeStruct((slots, width, hid), BF16),
            jax.ShapeDtypeStruct((slots, hid, 2 * feat), BF16),
        ],
        in_specs=[tile(width), tile(feat), weight(width, hid), weight(hid, 2 * feat)],
        out_specs=[tile(feat), tile(width), weight(width, hid), weight(hid, 2 * feat)],
        scratch_shapes=[
            pltpu.VMEM((rows, width), BF16),
            pltpu.VMEM((rows, hid), BF16),
            pltpu.VMEM((rows, 2 * feat), BF16),
            pltpu.VMEM((rows, hid), BF16),
        ],
        compiler_params=pltpu.CompilerParams(vmem_limit_bytes=LIMIT),
        cost_estimate=pl.CostEstimate(flops=11_000_000_000, bytes_accessed=12_000_000, transcendentals=0),
    )(mixed, cots, w_hidden, w_out)


def totals_body(nx, ny, nz, x_ref, o_ref, pair, part, landed, mine, deep, final, s_sem, r_sem, s2, r2, s3, r3, s4, r4, s5, r5):
    xi, yi, zi, ci = (lax.axis_index(n) for n in ("x", "y", "z", "c"))
    me = xi * ny + yi
    chips = nx * ny
    other = {"c": 1 - ci}
    barrier = pltpu.get_barrier_semaphore()
    pl.semaphore_signal(barrier, inc=1, device_id=other, device_id_type=MESH)
    for k in range(1, chips):
        pl.semaphore_signal(
            barrier, inc=1, device_id=place(nx, ny, lax.rem(me + k, chips), 1), device_id_type=MESH
        )
    for k in range(1, nz):
        pl.semaphore_signal(barrier, inc=1, device_id={"z": lax.rem(zi + k, nz)}, device_id_type=MESH)
    pl.semaphore_wait(barrier, 1 + chips - 1 + nz - 1)

    def remote(src, dst, send, recv, where):
        return pltpu.make_async_remote_copy(
            src_ref=src, dst_ref=dst, send_sem=send, recv_sem=recv, device_id=where, device_id_type=MESH
        )

    first = [
        remote(x_ref.at[(1 - ci) * chips + lax.rem(me + k, chips)], pair.at[lax.rem(me + k, chips)], s_sem.at[k], r_sem.at[k], other)
        for k in range(chips)
    ]
    for k in list(range(1, chips)) + [0]:
        first[k].start()
    spread = []
    for k in list(range(1, chips)) + [0]:
        first[k].wait()
        q = lax.rem(me + k, chips)
        summed = x_ref[ci * chips + q].astype(F32) + pair[q].astype(F32)
        if k:
            part[q] = summed.astype(BF16)
            spread.append(remote(part.at[q], landed.at[me], s2.at[k], r2.at[k], place(nx, ny, q, 1)))
            spread[-1].start()
        else:
            landed[me] = summed.astype(BF16)
    for copy in spread:
        copy.wait()
    total = landed[0].astype(F32)
    for q in range(1, chips):
        total += landed[q].astype(F32)
    mine[...] = total.astype(BF16)
    deep[zi] = total.astype(BF16)
    across = [
        remote(mine, deep.at[zi], s3.at[k], r3.at[k], {"z": lax.rem(zi + k, nz)}) for k in range(1, nz)
    ]
    for copy in across:
        copy.start()
    for copy in across:
        copy.wait()
    total = deep[0].astype(F32)
    for q in range(1, nz):
        total += deep[q].astype(F32)
    final[...] = total.astype(BF16)
    o_ref[ci * chips + me] = total.astype(BF16)
    back = [
        remote(final, o_ref.at[ci * chips + me], s4.at[k], r4.at[k], place(nx, ny, lax.rem(me + k, chips), 1))
        for k in range(1, chips)
    ]
    for copy in back:
        copy.start()
    shared = [remote(final, o_ref.at[ci * chips + me], s5.at[0], r5.at[0], other)]
    shared[0].start()
    for k in range(1, chips):
        back[k - 1].wait()
        q = ci * chips + lax.rem(me - k + chips, chips)
        shared.append(remote(o_ref.at[q], o_ref.at[q], s5.at[k], r5.at[k], other))
        shared[-1].start()
    for copy in shared:
        copy.wait()


def totals(packed, sizes, nz, ident):
    nx, ny = sizes
    pieces, depth, width = packed.shape
    chips = nx * ny
    dma = pltpu.SemaphoreType.DMA
    block = pltpu.VMEM((depth, width), BF16)
    return pl.pallas_call(
        functools.partial(totals_body, nx, ny, nz),
        out_shape=jax.ShapeDtypeStruct(packed.shape, BF16),
        in_specs=[VMEM],
        out_specs=VMEM,
        scratch_shapes=[
            pltpu.VMEM((chips, depth, width), BF16),
            pltpu.VMEM((chips, depth, width), BF16),
            pltpu.VMEM((chips, depth, width), BF16),
            block,
            pltpu.VMEM((nz, depth, width), BF16),
            block,
            dma((chips,)), dma((chips,)), dma((chips,)), dma((chips,)),
            dma((nz,)), dma((nz,)), dma((chips,)), dma((chips,)), dma((chips,)), dma((chips,)),
        ],
        compiler_params=pltpu.CompilerParams(
            collective_id=ident, has_side_effects=True, vmem_limit_bytes=16 * 1024 * 1024
        ),
        cost_estimate=pl.CostEstimate(flops=1_000_000_000, bytes_accessed=4_000_000, transcendentals=0),
    )(packed)


def summed_over_z(grads, nz):
    slots, rows, cols = grads.shape
    part = rows // nz
    z = lax.axis_index("z")
    down = [(i, (i - 1) % nz) for i in range(nz)]
    up = [(i, (i + 1) % nz) for i in range(nz)]

    def piece(offset, half):
        at = lax.rem(z + offset + nz, nz) * part
        return lax.dynamic_slice(grads, (half * (slots // 2), at, 0), (slots // 2, part, cols))

    one_down = lax.ppermute(piece(2, 0), "z", down)
    one_up = lax.ppermute(piece(2, 1), "z", up)
    side_down = lax.ppermute(piece(nz - 1, 1), "z", down)
    side_up = lax.ppermute(piece(1, 0), "z", up)
    two_down = lax.ppermute((one_down.astype(F32) + piece(nz - 1, 0).astype(F32)).astype(BF16), "z", down)
    two_up = lax.ppermute((one_up.astype(F32) + piece(1, 1).astype(F32)).astype(BF16), "z", up)
    low = piece(0, 0).astype(F32) + two_down.astype(F32) + side_up.astype(F32)
    high = piece(0, 1).astype(F32) + two_up.astype(F32) + side_down.astype(F32)
    return jnp.concatenate([low, high], axis=0).astype(BF16)


def both_cores(part):
    rows = part.shape[1]
    c = lax.axis_index("c")
    half = rows // 2
    kept = lax.dynamic_slice_in_dim(part, c * half, half, 1)
    sent = lax.dynamic_slice_in_dim(part, (1 - c) * half, half, 1)
    other = lax.ppermute(sent, "c", [(0, 1), (1, 0)])
    low = jnp.where(c == 0, kept, other)
    high = jnp.where(c == 0, other, kept)
    return jnp.concatenate([low, high], axis=0).transpose(1, 0, 2)


def per_device(spec, cotangent, widths, band_group, w_embed, w_qkv, w_proj, w_hidden, w_out):
    frames, cols = spec.shape
    feat, slot_count, width = w_embed.shape
    nx, ny, nz = (lax.axis_size(n) for n in ("x", "y", "z"))
    sizes = (nx, ny)
    groups = nx * ny
    peers = groups * 2
    pair = slot_count // 2
    each = frames // groups
    c = lax.axis_index("c")

    def own(w):
        return lax.dynamic_slice_in_dim(w, c * pair, pair, 1).transpose(1, 0, 2)

    we, wh, wo = own(w_embed), own(w_hidden), own(w_out)

    spec_rows, cot_rows = exchange(
        [spec.reshape(groups, each, cols), cotangent.reshape(groups, each, cols)], sizes, 1, 0
    )
    normed, cots, starts, slots = band_tiles(spec_rows, cot_rows, widths, band_group, groups, slot_count, feat)
    four = lambda a: a.reshape(peers, pair, *a.shape[1:])
    flat = lambda a: a.reshape(peers * pair, *a.shape[2:])
    normed, cots = exchange([four(normed), four(cots)], sizes, 2, 1)
    embedded = embed(normed, we)
    (tokens,) = exchange([embedded], sizes, 2, 2)
    mixed, *saved = attention_forward(flat(tokens), slots, w_qkv, w_proj)
    (mixed,) = exchange([four(mixed)], sizes, 2, 3)
    mask_tiles, dmix, grad_hidden, grad_out = tail(mixed, cots, wh, wo)
    grad_out = summed_over_z(grad_out, nz)
    grad_hidden = summed_over_z(grad_hidden, nz)
    dmix, mask_tiles = exchange([dmix, mask_tiles], sizes, 2, 4)
    dtok, sums = attention_backward(flat(dmix), slots, w_qkv, w_proj, saved, peers)
    mask = mask_rows(flat(mask_tiles), widths, starts, slots, groups, cols)
    (dtok,) = exchange([four(dtok)], sizes, 2, 5)
    (mask,) = exchange([mask], sizes, 1, 6)
    grad_embed = summed_over_z(embed_grad(normed, dtok), nz)
    sums = totals(sums, sizes, nz, 7)
    grad_qkv, grad_proj = plain(
        unpack_body,
        [jax.ShapeDtypeStruct(w_qkv.shape, F32), jax.ShapeDtypeStruct(w_proj.shape, F32)],
        [VMEM],
    )(sums)
    return (
        mask.reshape(frames, cols),
        both_cores(grad_embed),
        grad_qkv,
        grad_proj,
        both_cores(grad_hidden),
        both_cores(grad_out),
    )


def solution(mesh):
    split = Mesh(mesh.devices.reshape(4, 4, 4, 2), ("x", "y", "z", "c"))
    band = ("x", "y")
    tm = ("z", "c")
    placed = (
        P(tm, band),
        P(tm, band),
        P(),
        P(),
        P(None, band, None),
        P(),
        P(),
        P(None, band, None),
        P(None, band, None),
    )
    return jax.shard_map(
        per_device,
        mesh=split,
        in_specs=placed,
        out_specs=(
            P(tm, band),
            P(tm, band, None),
            P(),
            P(),
            P(tm, band, None),
            P(tm, band, None),
        ),
        check_vma=False,
    )
```

time: 522 us -> 328 us (0.63); the launches traced: 513 us -> 326 us
  waiting for transfers between devices: 260 us -> 35.6 us
  Pallas kernels: 0 us -> 223 us
  matrix products: 66.6 us -> 0 us
  blocking collectives: 46.4 us -> 0 us
  local copies, waits for them, and re-layouts: 81.6 us -> 40.8 us
  between operations: 17.5 us -> 1.07 us
  other arithmetic: 21.4 us -> 9.89 us
    pallas_call x0 -> x16, Pallas kernels: none -> 223 us  [the longest x7 114 us: exchange(): pl.pallas_call(functools.partial(exchange_body, nx, ny, cores, count), ou...]
    psum x1 -> x0, waiting for transfers between devices: 171 us -> none  [packed_total(): subtotal = lax.psum(jnp.concatenate([a.ravel() for a in arrays]), axis)]
    dot_general x22 -> x0, matrix products: 62.4 us -> none  [the longest x3 11.3 us: weight_grad(): jnp.einsum('fsa,fsb->asb', left, right, preferred_element_type=jnp.float32)]
    all_gather x1 -> x0, waiting for transfers between devices: 53.6 us -> none  [in_one_piece(): out = lax.all_gather(both, axis, axis=dim, tiled=True)]
    all_to_all x3 -> x0, blocking collectives: 46.4 us -> none  [the longest x1 16.2 us: per_device(): lax.all_to_all(mixed_shards, BAND, split_axis=1, concat_axis=0, tiled=True)]
    ppermute x0 -> x21, waiting for transfers between devices: none -> 35.6 us  [the longest x3 10.9 us: summed_over_z(): one_up = lax.ppermute(piece(2, 1), 'z', up)]
    reshape x13 -> x0, local copies, waits for them, and re-layouts: 27.7 us -> none  [the longest x3 9.84 us: cut_along(): shard.reshape(*lengths[:dim], peers, lengths[dim] // peers, *lengths[dim...]
    all_to_all x4 -> x0, waiting for transfers between devices: 26 us -> none  [the longest x3 13.1 us: sent_and_summed(): lax.all_to_all(cut_along(shard, dim, peers), axis, 0, 0, tiled=True)]
  transfers between devices with their start and end apart: 8 -> 21, of which waited for: 6 -> 9; matrix products, arithmetic and copies ran while one was open for 15% -> 5% of each run, Pallas kernels for 0% -> 18%
where the time goes in v1:
time: 328 us; the launch traced here: 326 us
  Pallas kernels  223 us (68%)
  local copies, waits for them, and re-layouts  40.8 us (12%)
  waiting for transfers between devices  35.6 us (11%)
  starting transfers between devices  16.1 us (5%)
  other arithmetic  9.89 us (3%)
    pallas_call x7, Pallas kernels, exchange(): pl.pallas_call(functools.partial(exchange_body, nx, ny, cores, count), ou...  114 us
    pallas_call x1, Pallas kernels, totals(): pl.pallas_call(functools.partial(totals_body, nx, ny, nz), out_shape=jax....  38.9 us
    unnamed x65, local copies, waits for them, and re-layouts  27.7 us
    pallas_call x1, Pallas kernels, attention_forward(): plain(forward_body, [jax.ShapeDtypeStruct(tokens.shape, BF16), jax.ShapeD...  17.7 us
    pallas_call x1, Pallas kernels, attention_backward(): plain(backward_body, [jax.ShapeDtypeStruct(grads.shape, BF16), jax.ShapeD...  16.4 us
    pallas_call x1, Pallas kernels, tail(): pl.pallas_call(tail_body, grid=(slots,), out_shape=[jax.ShapeDtypeStruct(...  15.4 us
    ppermute x3, waiting for transfers between devices, summed_over_z(): one_up = lax.ppermute(piece(2, 1), 'z', up)  10.9 us
    ppermute x3, waiting for transfers between devices, summed_over_z(): lax.ppermute((one_down.astype(F32) + piece(nz - 1, 0).astype(F32)).astype...  9.49 us
  transfers between devices with their start and end apart: 21, of which 9 were waited for; matrix products, arithmetic and copies ran while one was open for 5% of the time, Pallas kernels for 18%

profile of v1, /device:TPU:0, one launch (start us, length us, event | category | flops | bytes accessed | tf_op | source)
XLA Modules:
  0.0 326.2 jit_solution(10505684499929219675)
XLA Ops:
  0.7 1.1 copy-done
  4.8 11.3 %shard_map.136 = (bf16[16,16,256]{2,1,0:T(8,128)(2,1)S(1)}, bf16[16,16,256]{2,1,0:T(8,128)(2,1)S(1)}) custom-call(bf16[16,16,256]{2,1,0:T(8,128)(2,1)S(1)} %bitcast.28, bf16[16,16,256]{2,1,0:T(8,128)(2,1)S(1)} %bitcast.29), custom_call_target="tpu_custom_call" | custom-call | flops 1000000000 | bytes 4000000 | tf_op jit(solution)/shard_map/pallas_call | solution.py:84
  17.4 7.8 %shard_map.137 = (bf16[64,16,256]{2,1,0:T(8,128)(2,1)}, bf16[64,16,256]{2,1,0:T(8,128)(2,1)}, s32[32]{0:T(128)}, s32[32]{0:T(128)}) custom-call(bf16[16,16,256]{2,1,0:T(8,128)(2,1)} %copy-done.21, bf16[16,16,256]{2,1,0:T(8,128)(2,1)} %copy-done.22, s32[32]{0:T(128)} %widths_ref.3, s32[32]{0:T(128)} %group_ref.1), custom_call_target="tpu_custom_call" | custom-call | flops 1000000000 | bytes 4000000 | tf_op jit(solution)/shard_map/pallas_call | solution.py:149
  27.2 18.7 %shard_map.138 = (bf16[32,2,16,256]{3,2,1,0:T(8,128)(2,1)S(1)}, bf16[32,2,16,256]{3,2,1,0:T(8,128)(2,1)S(1)}) custom-call(bf16[32,2,16,256]{3,2,1,0:T(8,128)(2,1)S(1)} %bitcast.33, bf16[32,2,16,256]{3,2,1,0:T(8,128)(2,1)S(1)} %bitcast.34), custom_call_target="tpu_custom_call" | custom-call | flops 1000000000 | bytes 4000000 | tf_op jit(solution)/shard_map/pallas_call | solution.py:84
  47.5 2.5 shard_map.139.refs_0_
  50.0 1.1 copy-done.14
  51.1 15.7 %shard_map.140 = bf16[32,2,16,384]{3,2,1,0:T(8,128)(2,1)S(1)} custom-call(bf16[32,2,16,384]{3,2,1,0:T(8,128)(2,1)S(1)} %copy-done.14), custom_call_target="tpu_custom_call" | custom-call | flops 1000000000 | bytes 4000000 | tf_op jit(solution)/shard_map/pallas_call | solution.py:84
  67.7 17.7 %shard_map.141 = (bf16[64,16,384]{2,1,0:T(8,128)(2,1)}, bf16[512,384]{1,0:T(8,128)(2,1)}, bf16[512,1536]{1,0:T(8,128)(2,1)}, f32[8,512,128]{2,1,0:T(8,128)}, bf16[512,512]{1,0:T(8,128)(2,1)}) custom-call(bf16[64,16,384]{2,1,0:T(8,128)(2,1)} %bitcast.30, s32[32]{0:T(128)} %get-tuple-element.34.slots_ref, bf16[384,1536]{1,0:T(8,128)(2,1)} %w_qkv_ref.3, ...), custom_call_target="tpu_custom_call" | custom-call | flops 1000000000 | bytes 4000000 | tf_op jit(solution)/shard_map/pallas_call | solution.py:281
  85.3 1.1 copy-done.8
  86.5 17.3 %shard_map.142.mixed_ref = bf16[32,2,16,384]{3,2,1,0:T(8,128)(2,1)S(1)} custom-call(bf16[32,2,16,384]{3,2,1,0:T(8,128)(2,1)S(1)} %bitcast.31), custom_call_target="tpu_custom_call" | custom-call | flops 1000000000 | bytes 4000000 | tf_op jit(solution)/shard_map/pallas_call | solution.py:84
  104.7 4.9 %constant_dynamic-slice_fusion.13 = bf16[384,2,1536]{2,1,0:T(2,128)(2,1)S(1)} fusion(bf16[384,4,1536]{2,1,0:T(4,128)(2,1)} %param.16, s32[]{:T(128)S(6)} %select_n.107), kind=kLoop, calls=%fused_computation.55 | loop fusion | bytes 4718596 | tf_op jit(solution)/shard_map/dynamic_slice | solution.py:607
  109.6 1.6 copy.28
  111.2 3.3 %constant_dynamic-slice_fusion.12 = bf16[1536,2,512]{2,1,0:T(2,128)(2,1)S(1)} fusion(bf16[1536,4,512]{2,1,0:T(4,128)(2,1)S(1)} %bitcast.38, s32[]{:T(128)S(6)} %select_n.107), kind=kLoop, calls=%fused_computation.54 | loop fusion | bytes 6291460 | tf_op jit(solution)/shard_map/dynamic_slice | solution.py:607
  114.6 2.2 copy.27
  116.7 15.4 %shard_map.143 = (bf16[32,2,16,256]{3,2,1,0:T(8,128)(2,1)}, bf16[32,2,16,384]{3,2,1,0:T(8,128)(2,1)}, bf16[2,384,1536]{2,1,0:T(8,128)(2,1)}, bf16[2,1536,512]{2,1,0:T(8,128)(2,1)}) custom-call(bf16[32,2,16,384]{3,2,1,0:T(8,128)(2,1)} %copy-done.15, bf16[32,2,16,256]{3,2,1,0:T(8,128)(2,1)} %copy-done.19, bf16[2,384,1536]{2,1,0:T(8,128)(2,1)} %bitcast.36, ...), custom_call_target="tpu_custom_call" | custom-call | flops 11000000512 | bytes 12000000 | tf_op jit(solution)/shard_map/pallas_call | solution.py:438
  132.1 1.1 copy-done.16
  134.3 24.1 %shard_map.144 = (bf16[32,2,16,384]{3,2,1,0:T(8,128)(2,1)S(1)}, bf16[32,2,16,256]{3,2,1,0:T(8,128)(2,1)S(1)}) custom-call(bf16[32,2,16,384]{3,2,1,0:T(8,128)(2,1)S(1)} %copy-done.16, bf16[32,2,16,256]{3,2,1,0:T(8,128)(2,1)S(1)} %copy-done.18), custom_call_target="tpu_custom_call" | custom-call | flops 1000000000 | bytes 4000000 | tf_op jit(solution)/shard_map/pallas_call | solution.py:84
  160.1 16.4 %shard_map.147 = (bf16[64,16,384]{2,1,0:T(8,128)(2,1)}, bf16[32,64,384]{2,1,0:T(8,128)(2,1)}) custom-call(bf16[64,16,384]{2,1,0:T(8,128)(2,1)} %bitcast.25, s32[32]{0:T(128)} %get-tuple-element.34.slots_ref, bf16[384,1536]{1,0:T(8,128)(2,1)} %w_qkv_ref.3, bf16[512,384]{1,0:T(8,128)(2,1)} %w_proj_ref.3, bf16[512,384]{1,0:T(8,128)(2,1)} %get-tuple-element.42.rows_ref, ...), custom_call_target="tpu_custom_call" | custom-call | flops 1000000000 | bytes 4000000 | tf_op jit(solution)/shard_map/pallas_call | solution.py:360
  176.5 1.1 copy-done.4
  177.6 16.0 %shard_map.148.grad_ref = bf16[32,2,16,384]{3,2,1,0:T(8,128)(2,1)S(1)} custom-call(bf16[32,2,16,384]{3,2,1,0:T(8,128)(2,1)S(1)} %bitcast.27), custom_call_target="tpu_custom_call" | custom-call | flops 1000000000 | bytes 4000000 | tf_op jit(solution)/shard_map/pallas_call | solution.py:84
  194.5 2.7 shard_map.149
  198.1 2.0 collective-permute-start.2
  200.1 2.2 collective-permute-start.5
  202.3 3.2 collective-permute-start
  206.6 4.6 %shard_map.145.refs_0_ = bf16[16,16,256]{2,1,0:T(8,128)(2,1)} custom-call(bf16[64,16,256]{2,1,0:T(8,128)(2,1)} %bitcast.32, s32[32]{0:T(128)} %widths_ref.3, s32[32]{0:T(128)} %get-tuple-element.40.starts_ref, s32[32]{0:T(128)} %get-tuple-element.34.slots_ref), custom_call_target="tpu_custom_call" | custom-call | flops 1000000000 | bytes 4000000 | tf_op jit(solution)/shard_map/pallas_call | solution.py:181
  211.1 2.4 constant_dynamic-slice_fusion.1
  213.6 10.8 %shard_map.146 = bf16[16,16,256]{2,1,0:T(8,128)(2,1)S(1)} custom-call(bf16[16,16,256]{2,1,0:T(8,128)(2,1)S(1)} %copy-done.20), custom_call_target="tpu_custom_call" | custom-call | flops 1000000000 | bytes 4000000 | tf_op jit(solution)/shard_map/pallas_call | solution.py:84
  225.8 38.9 %shard_map.150.sums_ref = bf16[32,64,384]{2,1,0:T(8,128)(2,1)S(1)} custom-call(bf16[32,64,384]{2,1,0:T(8,128)(2,1)S(1)} %copy-done.3), custom_call_target="tpu_custom_call" | custom-call | flops 1000000000 | bytes 4000000 | tf_op jit(solution)/shard_map/pallas_call | solution.py:539
  264.8 1.2 copy-done.12
  266.2 1.8 collective-permute-start.10
  268.9 1.5 collective-permute-start.1
  270.4 3.1 shard_map.151
  273.6 3.5 %collective-permute-done.1 = bf16[1,64,384]{2,1,0:T(8,128)(2,1)S(1)} collective-permute-done((bf16[1,64,384]{2,1,0:T(8,128)(2,1)S(1)}, bf16[1,64,384]{2,1,0:T(8,128)(2,1)S(1)}, u32[]{:S(2)}, u32[]{:S(2)}) %collective-permute-start.1) | collective-permute-done | bytes 49184 | tf_op jit(solution)/shard_map/ppermute | solution.py:576
  279.3 10.9 %collective-permute-done.17 = bf16[1,384,512]{2,1,0:T(8,128)(2,1)S(1)} collective-permute-done((bf16[1,384,512]{2,1,0:T(8,128)(2,1)S(1)}, bf16[1,384,512]{2,1,0:T(8,128)(2,1)S(1)}, u32[]{:S(2)}, u32[]{:S(2)}) %collective-permute-start.17) | collective-permute-done | bytes 393248 | tf_op jit(solution)/shard_map/ppermute | solution.py:573
  290.5 1.1 add_convert_fusion.1
  291.7 2.0 collective-permute-start.18
  293.7 2.9 collective-permute-done.11
  296.6 1.1 add_convert_fusion.4
  298.7 3.5 %collective-permute-done.19 = bf16[1,384,512]{2,1,0:T(8,128)(2,1)S(1)} collective-permute-done((bf16[1,384,512]{2,1,0:T(8,128)(2,1)S(1)}, bf16[1,384,512]{2,1,0:T(8,128)(2,1)S(1)}, u32[]{:S(2)}, u32[]{:S(2)}) %collective-permute-start.19) | collective-permute-done | bytes 393248 | tf_op jit(solution)/shard_map/ppermute | solution.py:574
  302.2 8.4 %collective-permute-done.14 = bf16[1,384,512]{2,1,0:T(8,128)(2,1)S(1)} collective-permute-done((bf16[1,384,512]{2,1,0:T(8,128)(2,1)S(1)}, bf16[1,384,512]{2,1,0:T(8,128)(2,1)S(1)}, u32[]{:S(2)}, u32[]{:S(2)}) %collective-permute-start.14) | collective-permute-done | bytes 393248 | tf_op jit(solution)/shard_map/ppermute | solution.py:572
  310.7 1.4 add_convert_fusion
  312.0 1.5 collective-permute-start.15
  313.6 3.0 collective-permute-done.8
  316.6 1.1 add_convert_fusion.6
  317.8 3.0 collective-permute-done.15
  320.8 1.1 add_convert_fusion.2
  322.3 1.3 copy.19
  324.0 1.5 copy.20
  (100 shorter events, 23.1 us)
Async XLA Ops:
  0.6 1.1 copy-start
  3.0 0.9 copy-start.5
  3.9 0.9 copy-start.6
  25.1 1.0 copy-start.10
  26.2 1.0 copy-start.11
  45.9 0.8 copy-start.17
  46.7 0.8 copy-start.19
  50.0 1.1 copy-start.14
  66.8 0.9 copy-start.7
  85.3 1.1 copy-start.8
  86.5 24.8 %slice-start = ((s8[6291456]{0:T(1024)(128)(4,1)}), s8[4194304]{0:T(1024)(128)(4,1)S(1)}, s32[]{:S(2)}) async-start(s8[6291456]{0:T(1024)(128)(4,1)} %bitcast.37), calls=%async_computation | async-start | bytes 8388608
  103.8 0.9 copy-start.15
  104.7 6.6 %slice-start.1 = ((s8[6291456]{0:T(1024)(128)(4,1)}), s8[2097152]{0:T(1024)(128)(4,1)S(1)}, s32[]{:S(2)}) async-start(s8[6291456]{0:T(1024)(128)(4,1)} %bitcast.37), calls=%async_computation.1 | async-start | bytes 4194304
  132.1 1.1 copy-start.16
  133.3 1.0 copy-start.18
  158.4 0.9 copy-start.2
  159.3 0.8 copy-start.9
  176.5 1.1 copy-start.4
  193.6 0.9 copy-start.13
  194.5 11.0 %copy-start.23 = (bf16[2,384,1536]{2,1,0:T(8,128)(2,1)S(1)}, bf16[2,384,1536]{2,1,0:T(8,128)(2,1)}, u32[]{:S(2)}) copy-start(bf16[2,384,1536]{2,1,0:T(8,128)(2,1)} %get-tuple-element.50) | copy-start | bytes 7077892
  198.1 75.4 %collective-permute-start.2 = (bf16[1,64,384]{2,1,0:T(8,128)(2,1)S(1)}, bf16[1,64,384]{2,1,0:T(8,128)(2,1)S(1)}, u32[]{:S(2)}, u32[]{:S(2)}) collective-permute-start(bf16[1,64,384]{2,1,0:T(8,128)(2,1)S(1)} %get-tuple-element.78), channel_id=1, source_target_pairs={{0,2},{2,4},{4,6},{6,0},{1,3},{3,5},{5,7},{7,1},{8,10},{10,12},{12... | collective-permute-start | bytes 147464 | tf_op jit(solution)/shard_map/ppermute | solution.py:575
  200.1 65.9 %collective-permute-start.5 = (bf16[1,64,384]{2,1,0:T(8,128)(2,1)S(1)}, bf16[1,64,384]{2,1,0:T(8,128)(2,1)S(1)}, u32[]{:S(2)}, u32[]{:S(2)}) collective-permute-start(bf16[1,64,384]{2,1,0:T(8,128)(2,1)S(1)} %get-tuple-element.77), channel_id=1, source_target_pairs={{0,6},{2,0},{4,2},{6,4},{1,7},{3,1},{5,3},{7,5},{8,14},{10,8},{12,... | collective-permute-start | bytes 147464 | tf_op jit(solution)/shard_map/ppermute | solution.py:574
  202.3 22.1 %collective-permute-start.3 = (bf16[1,64,384]{2,1,0:T(8,128)(2,1)S(1)}, bf16[1,64,384]{2,1,0:T(8,128)(2,1)S(1)}, u32[]{:S(2)}, u32[]{:S(2)}) collective-permute-start(bf16[1,64,384]{2,1,0:T(8,128)(2,1)S(1)} %get-tuple-element.76), channel_id=1, source_target_pairs={{0,2},{2,4},{4,6},{6,0},{1,3},{3,5},{5,7},{7,1},{8,10},{10,12},{12... | collective-permute-start | bytes 147464 | tf_op jit(solution)/shard_map/ppermute | solution.py:573
  202.3 63.9 %collective-permute-start = (bf16[1,64,384]{2,1,0:T(8,128)(2,1)S(1)}, bf16[1,64,384]{2,1,0:T(8,128)(2,1)S(1)}, u32[]{:S(2)}, u32[]{:S(2)}) collective-permute-start(bf16[1,64,384]{2,1,0:T(8,128)(2,1)S(1)} %get-tuple-element.79), channel_id=1, source_target_pairs={{0,6},{2,0},{4,2},{6,4},{1,7},{3,1},{5,3},{7,5},{8,14},{10,8},{12,... | collective-permute-start | bytes 147464 | tf_op jit(solution)/shard_map/ppermute | solution.py:572
  206.6 107.0 %collective-permute-start.9 = (bf16[1,96,1536]{2,1,0:T(8,128)(2,1)}, bf16[1,96,1536]{2,1,0:T(8,128)(2,1)}, u32[]{:S(2)}, u32[]{:S(2)}) collective-permute-start(bf16[1,96,1536]{2,1,0:T(8,128)(2,1)} %get-tuple-element.68), channel_id=1, source_target_pairs={{0,2},{2,4},{4,6},{6,0},{1,3},{3,5},{5,7},{7,1},{8,10},{10,12},{12... | collective-permute-start | bytes 884744 | tf_op jit(solution)/shard_map/ppermute | solution.py:575
  211.1 2.4 copy-start.20
  213.6 12.2 %copy-start.3 = (bf16[32,64,384]{2,1,0:T(8,128)(2,1)S(1)}, bf16[32,64,384]{2,1,0:T(8,128)(2,1)}, u32[]{:S(2)}) copy-start(bf16[32,64,384]{2,1,0:T(8,128)(2,1)} %get-tuple-element.47.x_ref) | copy-start | bytes 4718596
  225.2 42.8 %collective-permute-start.4 = (bf16[1,64,384]{2,1,0:T(8,128)(2,1)S(1)}, bf16[1,64,384]{2,1,0:T(8,128)(2,1)S(1)}, u32[]{:S(2)}, u32[]{:S(2)}) collective-permute-start(bf16[1,64,384]{2,1,0:T(8,128)(2,1)S(1)} %add_convert_fusion.9), channel_id=1, source_target_pairs={{0,2},{2,4},{4,6},{6,0},{1,3},{3,5},{5,7},{7,1},{8,10},{10,12},{12... | collective-permute-start | bytes 147464 | tf_op jit(solution)/shard_map/ppermute | solution.py:577
  264.8 1.2 copy-start.12
  265.9 11.1 %copy-start.26 = (bf16[1,384,512]{2,1,0:T(8,128)(2,1)S(1)}, bf16[1,384,512]{2,1,0:T(8,128)(2,1)}, u32[]{:S(2)}) copy-start(bf16[1,384,512]{2,1,0:T(8,128)(2,1)} %get-tuple-element.60) | copy-start | bytes 1179652
  266.0 12.0 %copy-start.24 = (bf16[2,384,1536]{2,1,0:T(8,128)(2,1)S(1)}, bf16[2,384,1536]{2,1,0:T(8,128)(2,1)}, u32[]{:S(2)}) copy-start(bf16[2,384,1536]{2,1,0:T(8,128)(2,1)} %get-tuple-element.50) | copy-start | bytes 7077892
  266.0 25.6 %collective-permute-start.12 = (bf16[1,96,1536]{2,1,0:T(8,128)(2,1)}, bf16[1,96,1536]{2,1,0:T(8,128)(2,1)}, u32[]{:S(2)}, u32[]{:S(2)}) collective-permute-start(bf16[1,96,1536]{2,1,0:T(8,128)(2,1)} %get-tuple-element.67), channel_id=1, source_target_pairs={{0,6},{2,0},{4,2},{6,4},{1,7},{3,1},{5,3},{7,5},{8,14},{10,8},{12,... | collective-permute-start | bytes 884744 | tf_op jit(solution)/shard_map/ppermute | solution.py:574
  266.2 11.7 %collective-permute-start.10 = (bf16[1,96,1536]{2,1,0:T(8,128)(2,1)}, bf16[1,96,1536]{2,1,0:T(8,128)(2,1)}, u32[]{:S(2)}, u32[]{:S(2)}) collective-permute-start(bf16[1,96,1536]{2,1,0:T(8,128)(2,1)} %get-tuple-element.66), channel_id=1, source_target_pairs={{0,2},{2,4},{4,6},{6,0},{1,3},{3,5},{5,7},{7,1},{8,10},{10,12},{12... | collective-permute-start | bytes 884744 | tf_op jit(solution)/shard_map/ppermute | solution.py:573
  268.9 21.4 %copy-start.25 = (bf16[1,384,512]{2,1,0:T(8,128)(2,1)S(1)}, bf16[1,384,512]{2,1,0:T(8,128)(2,1)}, u32[]{:S(2)}) copy-start(bf16[1,384,512]{2,1,0:T(8,128)(2,1)} %get-tuple-element.61) | copy-start | bytes 1179652
  268.9 8.2 %collective-permute-start.1 = (bf16[1,64,384]{2,1,0:T(8,128)(2,1)S(1)}, bf16[1,64,384]{2,1,0:T(8,128)(2,1)S(1)}, u32[]{:S(2)}, u32[]{:S(2)}) collective-permute-start(bf16[1,64,384]{2,1,0:T(8,128)(2,1)S(1)} %get-tuple-element.75), channel_id=1, source_target_pairs={{0,6},{2,0},{4,2},{6,4},{1,7},{3,1},{5,3},{7,5},{8,14},{10,8},{12,... | collective-permute-start | bytes 147464 | tf_op jit(solution)/shard_map/ppermute | solution.py:576
  273.5 18.2 %collective-permute-start.7 = (bf16[1,96,1536]{2,1,0:T(8,128)(2,1)}, bf16[1,96,1536]{2,1,0:T(8,128)(2,1)S(1)}, u32[]{:S(2)}, u32[]{:S(2)}) collective-permute-start(bf16[1,96,1536]{2,1,0:T(8,128)(2,1)} %get-tuple-element.69), channel_id=1, source_target_pairs={{0,6},{2,0},{4,2},{6,4},{1,7},{3,1},{5,3},{7,5},{8,14},{10,8},{12,... | collective-permute-start | bytes 884744 | tf_op jit(solution)/shard_map/ppermute | solution.py:572
  277.0 13.2 %collective-permute-start.17 = (bf16[1,384,512]{2,1,0:T(8,128)(2,1)S(1)}, bf16[1,384,512]{2,1,0:T(8,128)(2,1)S(1)}, u32[]{:S(2)}, u32[]{:S(2)}) collective-permute-start(bf16[1,384,512]{2,1,0:T(8,128)(2,1)S(1)} %copy-done.26), channel_id=1, source_target_pairs={{0,2},{2,4},{4,6},{6,0},{1,3},{3,5},{5,7},{7,1},{8,10},{10,12},{12... | collective-permute-start | bytes 1179656 | tf_op jit(solution)/shard_map/ppermute | solution.py:573
  277.9 1.3 collective-permute-start.6
  279.2 17.3 %collective-permute-start.11 = (bf16[1,96,1536]{2,1,0:T(8,128)(2,1)S(1)}, bf16[1,96,1536]{2,1,0:T(8,128)(2,1)S(1)}, u32[]{:S(2)}, u32[]{:S(2)}) collective-permute-start(bf16[1,96,1536]{2,1,0:T(8,128)(2,1)S(1)} %add_convert_fusion.5), channel_id=1, source_target_pairs={{0,2},{2,4},{4,6},{6,0},{1,3},{3,5},{5,7},{7,1},{8,10},{10,12},{12... | collective-permute-start | bytes 884744 | tf_op jit(solution)/shard_map/ppermute | solution.py:577
  290.2 12.0 %collective-permute-start.19 = (bf16[1,384,512]{2,1,0:T(8,128)(2,1)S(1)}, bf16[1,384,512]{2,1,0:T(8,128)(2,1)S(1)}, u32[]{:S(2)}, u32[]{:S(2)}) collective-permute-start(bf16[1,384,512]{2,1,0:T(8,128)(2,1)S(1)} %copy-done.25), channel_id=1, source_target_pairs={{0,6},{2,0},{4,2},{6,4},{1,7},{3,1},{5,3},{7,5},{8,14},{10,8},{12,... | collective-permute-start | bytes 1179656 | tf_op jit(solution)/shard_map/ppermute | solution.py:574
  291.6 19.1 %collective-permute-start.14 = (bf16[1,384,512]{2,1,0:T(8,128)(2,1)S(1)}, bf16[1,384,512]{2,1,0:T(8,128)(2,1)S(1)}, u32[]{:S(2)}, u32[]{:S(2)}) collective-permute-start(bf16[1,384,512]{2,1,0:T(8,128)(2,1)S(1)} %get-tuple-element.63), channel_id=1, source_target_pairs={{0,6},{2,0},{4,2},{6,4},{1,7},{3,1},{5,3},{7,5},{8,14},{10,8},{12,... | collective-permute-start | bytes 1179656 | tf_op jit(solution)/shard_map/ppermute | solution.py:572
  291.7 19.0 %collective-permute-start.18 = (bf16[1,384,512]{2,1,0:T(8,128)(2,1)S(1)}, bf16[1,384,512]{2,1,0:T(8,128)(2,1)S(1)}, u32[]{:S(2)}, u32[]{:S(2)}) collective-permute-start(bf16[1,384,512]{2,1,0:T(8,128)(2,1)S(1)} %add_convert_fusion.1), channel_id=1, source_target_pairs={{0,2},{2,4},{4,6},{6,0},{1,3},{3,5},{5,7},{7,1},{8,10},{10,12},{12... | collective-permute-start | bytes 1179656 | tf_op jit(solution)/shard_map/ppermute | solution.py:577
  297.7 18.9 %collective-permute-start.8 = (bf16[1,96,1536]{2,1,0:T(8,128)(2,1)S(1)}, bf16[1,96,1536]{2,1,0:T(8,128)(2,1)S(1)}, u32[]{:S(2)}, u32[]{:S(2)}) collective-permute-start(bf16[1,96,1536]{2,1,0:T(8,128)(2,1)S(1)} %get-tuple-element.65), channel_id=1, source_target_pairs={{0,6},{2,0},{4,2},{6,4},{1,7},{3,1},{5,3},{7,5},{8,14},{10,8},{12,... | collective-permute-start | bytes 884744 | tf_op jit(solution)/shard_map/ppermute | solution.py:576
  302.2 15.5 %collective-permute-start.16 = (bf16[1,384,512]{2,1,0:T(8,128)(2,1)}, bf16[1,384,512]{2,1,0:T(8,128)(2,1)S(1)}, u32[]{:S(2)}, u32[]{:S(2)}) collective-permute-start(bf16[1,384,512]{2,1,0:T(8,128)(2,1)} %get-tuple-element.62), channel_id=1, source_target_pairs={{0,2},{2,4},{4,6},{6,0},{1,3},{3,5},{5,7},{7,1},{8,10},{10,12},{12... | collective-permute-start | bytes 1179656 | tf_op jit(solution)/shard_map/ppermute | solution.py:575
  312.0 8.7 %collective-permute-start.15 = (bf16[1,384,512]{2,1,0:T(8,128)(2,1)S(1)}, bf16[1,384,512]{2,1,0:T(8,128)(2,1)S(1)}, u32[]{:S(2)}, u32[]{:S(2)}) collective-permute-start(bf16[1,384,512]{2,1,0:T(8,128)(2,1)S(1)} %get-tuple-element.59), channel_id=1, source_target_pairs={{0,6},{2,0},{4,2},{6,4},{1,7},{3,1},{5,3},{7,5},{8,14},{10,8},{12,... | collective-permute-start | bytes 1179656 | tf_op jit(solution)/shard_map/ppermute | solution.py:576
  317.7 4.4 %collective-permute-start.13 = (bf16[2,48,1536]{2,1,0:T(8,128)(2,1)S(1)}, bf16[2,48,1536]{2,1,0:T(8,128)(2,1)S(1)}, u32[]{:S(2)}, u32[]{:S(2)}) collective-permute-start(bf16[2,48,1536]{2,1,0:T(8,128)(2,1)S(1)} %fusion.2), channel_id=1, source_target_pairs={{0,1},{1,0},{2,3},{3,2},{4,5},{5,4},{6,7},{7,6},{8,9},{9,8},{10,11... | collective-permute-start | bytes 884744 | tf_op jit(solution)/shard_map/ppermute | solution.py:589
  322.0 1.8 collective-permute-start.20
  322.3 3.9 %copy-start.1 = (bf16[256,4,384]{2,1,0:T(4,128)(2,1)S(1)}, bf16[256,4,384]{2,1,0:T(4,128)(2,1)}, u32[]{:S(2)}) copy-start(bf16[256,4,384]{2,1,0:T(4,128)(2,1)} %param.13) | copy-start | bytes 2359300
  (2 other events, 1.3 us)

commit v2 on v1

--- a/solution.py
+++ b/solution.py
@@ -15,22 +15,21 @@
 F32 = jnp.float32
 VMEM = pl.BlockSpec(memory_space=pltpu.VMEM)
 SMEM = pl.BlockSpec(memory_space=pltpu.SMEM)
-LIMIT = 60 * 1024 * 1024
+MIB = 1024 * 1024
 
 
 def dot(a, b, da, db):
     return lax.dot_general(a, b, (((da,), (db,)), ((), ())), preferred_element_type=F32)
 
 
-def plain(body, outs, ins, scratch=(), flops=1_000_000_000, out_specs=None):
+def plain(body, outs, ins, scratch=(), mib=8, out_specs=None):
     return pl.pallas_call(
         body,
         out_shape=outs,
         in_specs=ins,
         out_specs=out_specs if out_specs is not None else [VMEM] * len(outs),
         scratch_shapes=scratch,
-        compiler_params=pltpu.CompilerParams(vmem_limit_bytes=LIMIT),
-        cost_estimate=pl.CostEstimate(flops=flops, bytes_accessed=4_000_000, transcendentals=0),
+        compiler_params=pltpu.CompilerParams(vmem_limit_bytes=mib * MIB),
     )
 
 
@@ -94,7 +93,6 @@
         compiler_params=pltpu.CompilerParams(
             collective_id=ident, has_side_effects=True, vmem_limit_bytes=16 * 1024 * 1024
         ),
-        cost_estimate=pl.CostEstimate(flops=1_000_000_000, bytes_accessed=4_000_000, transcendentals=0),
     )(*arrays)
 
 
@@ -116,14 +114,20 @@
     window = feat + 128
     lane = lax.broadcasted_iota(jnp.int32, (frames, feat), 1)
 
-    def step(b, start):
-        width = widths_ref[b]
+    def index(b, start):
         group = group_ref[b]
         rank = counts[group]
         counts[group] = rank + 1
-        slot = group * slot_count + rank
         starts_ref[b] = start
-        slots_ref[b] = slot
+        slots_ref[b] = group * slot_count + rank
+        return start + widths_ref[b]
+
+    lax.fori_loop(0, bands, index, jnp.int32(0))
+
+    def step(b, carry):
+        width = widths_ref[b]
+        slot = slots_ref[b]
+        start = starts_ref[b]
         offset = 4 * start
         base = pl.multiple_of((offset // 128) * 128, 128)
         shift = lax.rem(window - (offset - base), window)
@@ -136,9 +140,9 @@
         mean = jnp.sum(raw * raw, axis=1, keepdims=True) / counted
         normed_ref[slot] = (raw * lax.rsqrt(mean + EPSILON)).astype(BF16)
         cots_ref[slot] = cot.astype(BF16)
-        return start + width
-
-    lax.fori_loop(0, bands, step, jnp.int32(0))
+        return carry
+
+    lax.fori_loop(0, bands, step, 0, unroll=4)
 
 
 def band_tiles(spec_rows, cot_rows, widths, band_group, groups, slot_count, feat):
@@ -289,6 +293,7 @@
         ],
         [VMEM, SMEM, VMEM, VMEM],
         [pltpu.VMEM((bands, frames, width), BF16)],
+        mib=14,
     )(tokens, slots, w_qkv, w_proj)
 
 
@@ -369,6 +374,7 @@
             pltpu.VMEM((rows, inner), BF16),
             pltpu.VMEM((rows, 3 * inner), BF16),
         ],
+        mib=20,
     )(grads, slots, w_qkv, w_proj, *saved)
 
 
@@ -452,49 +458,179 @@
             pltpu.VMEM((rows, 2 * feat), BF16),
             pltpu.VMEM((rows, hid), BF16),
         ],
-        compiler_params=pltpu.CompilerParams(vmem_limit_bytes=LIMIT),
-        cost_estimate=pl.CostEstimate(flops=11_000_000_000, bytes_accessed=12_000_000, transcendentals=0),
+        compiler_params=pltpu.CompilerParams(vmem_limit_bytes=24 * MIB),
     )(mixed, cots, w_hidden, w_out)
 
 
-def totals_body(nx, ny, nz, x_ref, o_ref, pair, part, landed, mine, deep, final, s_sem, r_sem, s2, r2, s3, r3, s4, r4, s5, r5):
+def remote(src, dst, send, recv, where):
+    return pltpu.make_async_remote_copy(
+        src_ref=src, dst_ref=dst, send_sem=send, recv_sem=recv, device_id=where, device_id_type=MESH
+    )
+
+
+def rows_of(ref, slot, step, nz):
+    part = ref.shape[1] // nz
+    at = lax.rem(lax.axis_index("z") + step + nz, nz) * part
+    return ref.at[slot, pl.ds(pl.multiple_of(at, part), part)]
+
+
+def z_place(step, nz):
+    return {"z": lax.rem(lax.axis_index("z") + step + nz, nz)}
+
+
+def far_sends(ref, down, up, send, recv, nz):
+    return [
+        remote(rows_of(ref, 0, 2, nz), down, send.at[0], recv.at[0], z_place(-1, nz)),
+        remote(rows_of(ref, 1, 2, nz), up, send.at[1], recv.at[1], z_place(1, nz)),
+    ]
+
+
+def side_sends(ref, down, up, send, recv, nz):
+    return [
+        remote(rows_of(ref, 1, -1, nz), down, send.at[0], recv.at[0], z_place(-1, nz)),
+        remote(rows_of(ref, 0, 1, nz), up, send.at[1], recv.at[1], z_place(1, nz)),
+    ]
+
+
+def near_sends(down_src, up_src, down, up, send, recv, nz):
+    return [
+        remote(down_src, down, send.at[0], recv.at[0], z_place(-1, nz)),
+        remote(up_src, up, send.at[1], recv.at[1], z_place(1, nz)),
+    ]
+
+
+def add_own(ref, received, out, slot, step, nz):
+    out[...] = (received[...].astype(F32) + rows_of(ref, slot, step, nz)[...].astype(F32)).astype(BF16)
+
+
+def spread_body(nx, ny, nz, *refs):
+    (dmix, tiles, go, gh, o_dmix, o_tiles, o_down, o_up, h_down, h_up) = refs[:10]
+    (ro_down, ro_up, rh_down, rh_up, send, recv, local, zs, zr) = refs[10:]
+    me = (lax.axis_index("x") * ny + lax.axis_index("y")) * 2 + lax.axis_index("c")
+    peers = nx * ny * 2
+    barrier = pltpu.get_barrier_semaphore()
+    for k in range(1, peers):
+        pl.semaphore_signal(
+            barrier, inc=1, device_id=place(nx, ny, lax.rem(me + k, peers), 2), device_id_type=MESH
+        )
+    for step in (-1, 1):
+        pl.semaphore_signal(barrier, inc=1, device_id=z_place(step, nz), device_id_type=MESH)
+    pl.semaphore_wait(barrier, peers - 1 + 2)
+    first = far_sends(go, ro_down, ro_up, zs.at[0], zr.at[0], nz)
+    second = far_sends(gh, rh_down, rh_up, zs.at[1], zr.at[1], nz)
+    copies = []
+    for copy in first + second:
+        copy.start()
+    for a, (src, dst) in enumerate(((dmix, o_dmix), (tiles, o_tiles))):
+        for k in range(1, peers):
+            peer = lax.rem(me + k, peers)
+            copies.append(
+                remote(src.at[peer], dst.at[me], send.at[a, k], recv.at[a, k], place(nx, ny, peer, 2))
+            )
+            copies[-1].start()
+    own = [
+        pltpu.make_async_copy(dmix.at[me], o_dmix.at[me], local.at[0]),
+        pltpu.make_async_copy(tiles.at[me], o_tiles.at[me], local.at[1]),
+    ]
+    for copy in own:
+        copy.start()
+    for copy in first + second:
+        copy.wait()
+    add_own(go, ro_down, o_down, 0, -1, nz)
+    add_own(go, ro_up, o_up, 1, 1, nz)
+    add_own(gh, rh_down, h_down, 0, -1, nz)
+    add_own(gh, rh_up, h_up, 1, 1, nz)
+    for copy in own + copies:
+        copy.wait()
+
+
+def spread(dmix, tiles, go, gh, sizes, nz, ident):
+    peers = dmix.shape[0]
+    shape_o = (go.shape[1] // nz, go.shape[2])
+    shape_h = (gh.shape[1] // nz, gh.shape[2])
+    dma = pltpu.SemaphoreType.DMA
+    out = [jax.ShapeDtypeStruct(a, BF16) for a in (dmix.shape, tiles.shape, shape_o, shape_o, shape_h, shape_h)]
+    return pl.pallas_call(
+        functools.partial(spread_body, *sizes, nz),
+        out_shape=out,
+        in_specs=[VMEM] * 4,
+        out_specs=[VMEM] * 6,
+        scratch_shapes=[pltpu.VMEM(a, BF16) for a in (shape_o, shape_o, shape_h, shape_h)]
+        + [dma((2, peers)), dma((2, peers)), dma((2,)), dma((2, 2)), dma((2, 2))],
+        compiler_params=pltpu.CompilerParams(
+            collective_id=ident, has_side_effects=True, vmem_limit_bytes=8 * 1024 * 1024
+        ),
+    )(dmix, tiles, go, gh)
+
+
+def finish_body(nx, ny, nz, *refs):
+    (x_ref, dtok, mask, normed, go, gh, so_down, so_up, sh_down, sh_up) = refs[:10]
+    (o_ref, e_out, out_o, out_h, mask_out) = refs[10:15]
+    (pair, part, landed, mine, deep, final, dgrad, ge, e_one_d, e_one_u, e_src_d, e_src_u) = refs[15:27]
+    sides, nears = refs[27:33], refs[33:39]
+    swaps = refs[39:42]
+    (s1, r1, s2, r2, s3, r3, s4, r4, s5, r5, sd, rd, sm, rm, zs, zr, sw, rw, local) = refs[42:]
     xi, yi, zi, ci = (lax.axis_index(n) for n in ("x", "y", "z", "c"))
     me = xi * ny + yi
     chips = nx * ny
+    peers = chips * 2
+    who = me * 2 + ci
     other = {"c": 1 - ci}
     barrier = pltpu.get_barrier_semaphore()
-    pl.semaphore_signal(barrier, inc=1, device_id=other, device_id_type=MESH)
-    for k in range(1, chips):
+    for k in range(1, peers):
         pl.semaphore_signal(
-            barrier, inc=1, device_id=place(nx, ny, lax.rem(me + k, chips), 1), device_id_type=MESH
+            barrier, inc=1, device_id=place(nx, ny, lax.rem(who + k, peers), 2), device_id_type=MESH
         )
     for k in range(1, nz):
         pl.semaphore_signal(barrier, inc=1, device_id={"z": lax.rem(zi + k, nz)}, device_id_type=MESH)
-    pl.semaphore_wait(barrier, 1 + chips - 1 + nz - 1)
-
-    def remote(src, dst, send, recv, where):
-        return pltpu.make_async_remote_copy(
-            src_ref=src, dst_ref=dst, send_sem=send, recv_sem=recv, device_id=where, device_id_type=MESH
+    pl.semaphore_wait(barrier, peers - 1 + nz - 1)
+
+    first = [
+        remote(
+            x_ref.at[(1 - ci) * chips + lax.rem(me + k, chips)],
+            pair.at[lax.rem(me + k, chips)],
+            s1.at[k],
+            r1.at[k],
+            other,
         )
-
-    first = [
-        remote(x_ref.at[(1 - ci) * chips + lax.rem(me + k, chips)], pair.at[lax.rem(me + k, chips)], s_sem.at[k], r_sem.at[k], other)
         for k in range(chips)
     ]
     for k in list(range(1, chips)) + [0]:
         first[k].start()
-    spread = []
+    near = near_sends(so_down, so_up, nears[0], nears[1], zs.at[0], zr.at[0], nz)
+    near += near_sends(sh_down, sh_up, nears[2], nears[3], zs.at[1], zr.at[1], nz)
+    near += side_sends(go, sides[0], sides[1], zs.at[2], zr.at[2], nz)
+    near += side_sends(gh, sides[2], sides[3], zs.at[3], zr.at[3], nz)
+    for copy in near:
+        copy.start()
+    rest = []
+    for k in range(1, chips):
+        q = lax.rem(me + k, chips)
+        rest.append(remote(mask.at[q], mask_out.at[me], sm.at[k], rm.at[k], place(nx, ny, q, 1)))
+        rest[-1].start()
+    own = [
+        pltpu.make_async_copy(mask.at[me], mask_out.at[me], local.at[0]),
+        pltpu.make_async_copy(dtok.at[who], dgrad.at[who], local.at[1]),
+    ]
+    for copy in own:
+        copy.start()
+    spread_sums = []
     for k in list(range(1, chips)) + [0]:
         first[k].wait()
         q = lax.rem(me + k, chips)
-        summed = x_ref[ci * chips + q].astype(F32) + pair[q].astype(F32)
+        summed = (x_ref[ci * chips + q].astype(F32) + pair[q].astype(F32)).astype(BF16)
         if k:
-            part[q] = summed.astype(BF16)
-            spread.append(remote(part.at[q], landed.at[me], s2.at[k], r2.at[k], place(nx, ny, q, 1)))
-            spread[-1].start()
+            part[q] = summed
+            spread_sums.append(remote(part.at[q], landed.at[me], s2.at[k], r2.at[k], place(nx, ny, q, 1)))
+            spread_sums[-1].start()
         else:
-            landed[me] = summed.astype(BF16)
-    for copy in spread:
+            landed[me] = summed
+    grads = []
+    for k in range(1, peers):
+        peer = lax.rem(who + k, peers)
+        grads.append(remote(dtok.at[peer], dgrad.at[who], sd.at[k], rd.at[k], place(nx, ny, peer, 2)))
+        grads[-1].start()
+    for copy in spread_sums:
         copy.wait()
     total = landed[0].astype(F32)
     for q in range(1, chips):
@@ -513,83 +649,103 @@
         total += deep[q].astype(F32)
     final[...] = total.astype(BF16)
     o_ref[ci * chips + me] = total.astype(BF16)
-    back = [
-        remote(final, o_ref.at[ci * chips + me], s4.at[k], r4.at[k], place(nx, ny, lax.rem(me + k, chips), 1))
-        for k in range(1, chips)
-    ]
-    for copy in back:
-        copy.start()
+    back = []
+    for k in range(1, chips):
+        back.append(
+            remote(final, o_ref.at[ci * chips + me], s4.at[k], r4.at[k], place(nx, ny, lax.rem(me + k, chips), 1))
+        )
+        back[-1].start()
     shared = [remote(final, o_ref.at[ci * chips + me], s5.at[0], r5.at[0], other)]
     shared[0].start()
+
+    def split(grad, near_d, near_u, side_d, side_u, out, swap, job):
+        half = out.shape[2]
+        for slot, (a, b) in enumerate(((near_d, side_u), (near_u, side_d))):
+            own_rows = rows_of(grad, slot, 0, nz)[...].astype(F32)
+            rows = (own_rows + a[...].astype(F32) + b[...].astype(F32)).astype(BF16)
+            low, high = rows[:half], rows[half:]
+            out[ci, slot] = jnp.where(ci == 0, low, high)
+            swap[slot] = jnp.where(ci == 0, high, low)
+        rest.append(remote(swap, out.at[ci], sw.at[job], rw.at[job], other))
+        rest[-1].start()
+
+    for copy in own + grads:
+        copy.wait()
+    _, slots, frames, feat = normed.shape
+    for s in range(slots):
+        left = normed[:, s].reshape(peers * frames, feat)
+        right = dgrad[:, s].reshape(peers * frames, dgrad.shape[3])
+        ge[s] = dot(left, right, 0, 0).astype(BF16)
+    e_far = far_sends(ge, e_one_d, e_one_u, zs.at[4], zr.at[4], nz)
+    e_side = side_sends(ge, sides[4], sides[5], zs.at[5], zr.at[5], nz)
+    for copy in e_far + e_side:
+        copy.start()
+    for copy in near:
+        copy.wait()
+    split(go, nears[0], nears[1], sides[0], sides[1], out_o, swaps[0], 0)
+    split(gh, nears[2], nears[3], sides[2], sides[3], out_h, swaps[1], 1)
+    for copy in e_far:
+        copy.wait()
+    add_own(ge, e_one_d, e_src_d, 0, -1, nz)
+    add_own(ge, e_one_u, e_src_u, 1, 1, nz)
+    e_near = near_sends(e_src_d, e_src_u, nears[4], nears[5], zs.at[6], zr.at[6], nz)
+    for copy in e_near:
+        copy.start()
+    for copy in e_side + e_near:
+        copy.wait()
+    split(ge, nears[4], nears[5], sides[4], sides[5], e_out, swaps[2], 2)
     for k in range(1, chips):
         back[k - 1].wait()
         q = ci * chips + lax.rem(me - k + chips, chips)
         shared.append(remote(o_ref.at[q], o_ref.at[q], s5.at[k], r5.at[k], other))
         shared[-1].start()
-    for copy in shared:
-        copy.wait()
-
-
-def totals(packed, sizes, nz, ident):
+    for copy in rest + shared:
+        copy.wait()
+
+
+def finish(packed, dtok, mask, normed, go, gh, srcs, sizes, nz, ident):
     nx, ny = sizes
     pieces, depth, width = packed.shape
     chips = nx * ny
+    peers = dtok.shape[0]
+    slots, feat = normed.shape[1], normed.shape[3]
     dma = pltpu.SemaphoreType.DMA
-    block = pltpu.VMEM((depth, width), BF16)
+
+    def vmem(*shape):
+        return pltpu.VMEM(shape, BF16)
+
+    def parts(rows, cols):
+        return vmem(rows // nz, cols)
+
+    dims = [(go.shape[1], go.shape[2]), (gh.shape[1], gh.shape[2]), (feat, width)]
+    halves = [(slots, r // nz // 2, c) for r, c in dims]
+    block = vmem(depth, width)
+    each = [parts(*d) for d in dims for _ in range(2)]
+    scratch = [
+        vmem(chips, depth, width), vmem(chips, depth, width), vmem(chips, depth, width),
+        block, vmem(nz, depth, width), block,
+        vmem(*dtok.shape), vmem(slots, feat, width),
+    ]
+    scratch += [parts(feat, width) for _ in range(4)]
+    scratch += each + each + [vmem(*h) for h in halves]
+    scratch += [dma((chips,)) for _ in range(4)] + [dma((nz,)) for _ in range(2)] + [dma((chips,)) for _ in range(4)]
+    scratch += [dma((peers,)), dma((peers,)), dma((chips,)), dma((chips,))]
+    scratch += [dma((7, 2)), dma((7, 2)), dma((3,)), dma((3,)), dma((2,))]
+    outs = [packed.shape, (2, *halves[2]), (2, *halves[0]), (2, *halves[1]), mask.shape]
     return pl.pallas_call(
-        functools.partial(totals_body, nx, ny, nz),
-        out_shape=jax.ShapeDtypeStruct(packed.shape, BF16),
-        in_specs=[VMEM],
-        out_specs=VMEM,
-        scratch_shapes=[
-            pltpu.VMEM((chips, depth, width), BF16),
-            pltpu.VMEM((chips, depth, width), BF16),
-            pltpu.VMEM((chips, depth, width), BF16),
-            block,
-            pltpu.VMEM((nz, depth, width), BF16),
-            block,
-            dma((chips,)), dma((chips,)), dma((chips,)), dma((chips,)),
-            dma((nz,)), dma((nz,)), dma((chips,)), dma((chips,)), dma((chips,)), dma((chips,)),
-        ],
+        functools.partial(finish_body, nx, ny, nz),
+        out_shape=[jax.ShapeDtypeStruct(o, BF16) for o in outs],
+        in_specs=[VMEM] * 10,
+        out_specs=[VMEM] * 5,
+        scratch_shapes=scratch,
         compiler_params=pltpu.CompilerParams(
-            collective_id=ident, has_side_effects=True, vmem_limit_bytes=16 * 1024 * 1024
+            collective_id=ident, has_side_effects=True, vmem_limit_bytes=20 * 1024 * 1024
         ),
-        cost_estimate=pl.CostEstimate(flops=1_000_000_000, bytes_accessed=4_000_000, transcendentals=0),
-    )(packed)
-
-
-def summed_over_z(grads, nz):
-    slots, rows, cols = grads.shape
-    part = rows // nz
-    z = lax.axis_index("z")
-    down = [(i, (i - 1) % nz) for i in range(nz)]
-    up = [(i, (i + 1) % nz) for i in range(nz)]
-
-    def piece(offset, half):
-        at = lax.rem(z + offset + nz, nz) * part
-        return lax.dynamic_slice(grads, (half * (slots // 2), at, 0), (slots // 2, part, cols))
-
-    one_down = lax.ppermute(piece(2, 0), "z", down)
-    one_up = lax.ppermute(piece(2, 1), "z", up)
-    side_down = lax.ppermute(piece(nz - 1, 1), "z", down)
-    side_up = lax.ppermute(piece(1, 0), "z", up)
-    two_down = lax.ppermute((one_down.astype(F32) + piece(nz - 1, 0).astype(F32)).astype(BF16), "z", down)
-    two_up = lax.ppermute((one_up.astype(F32) + piece(1, 1).astype(F32)).astype(BF16), "z", up)
-    low = piece(0, 0).astype(F32) + two_down.astype(F32) + side_up.astype(F32)
-    high = piece(0, 1).astype(F32) + two_up.astype(F32) + side_down.astype(F32)
-    return jnp.concatenate([low, high], axis=0).astype(BF16)
-
-
-def both_cores(part):
-    rows = part.shape[1]
-    c = lax.axis_index("c")
-    half = rows // 2
-    kept = lax.dynamic_slice_in_dim(part, c * half, half, 1)
-    sent = lax.dynamic_slice_in_dim(part, (1 - c) * half, half, 1)
-    other = lax.ppermute(sent, "c", [(0, 1), (1, 0)])
-    low = jnp.where(c == 0, kept, other)
-    high = jnp.where(c == 0, other, kept)
-    return jnp.concatenate([low, high], axis=0).transpose(1, 0, 2)
+    )(packed, dtok, mask, normed, go, gh, *srcs)
+
+
+def interleaved(halves):
+    return halves.reshape(-1, *halves.shape[2:]).transpose(1, 0, 2)
 
 
 def per_device(spec, cotangent, widths, band_group, w_embed, w_qkv, w_proj, w_hidden, w_out):
@@ -620,15 +776,12 @@
     mixed, *saved = attention_forward(flat(tokens), slots, w_qkv, w_proj)
     (mixed,) = exchange([four(mixed)], sizes, 2, 3)
     mask_tiles, dmix, grad_hidden, grad_out = tail(mixed, cots, wh, wo)
-    grad_out = summed_over_z(grad_out, nz)
-    grad_hidden = summed_over_z(grad_hidden, nz)
-    dmix, mask_tiles = exchange([dmix, mask_tiles], sizes, 2, 4)
+    dmix, mask_tiles, *srcs = spread(dmix, mask_tiles, grad_out, grad_hidden, sizes, nz, 4)
     dtok, sums = attention_backward(flat(dmix), slots, w_qkv, w_proj, saved, peers)
     mask = mask_rows(flat(mask_tiles), widths, starts, slots, groups, cols)
-    (dtok,) = exchange([four(dtok)], sizes, 2, 5)
-    (mask,) = exchange([mask], sizes, 1, 6)
-    grad_embed = summed_over_z(embed_grad(normed, dtok), nz)
-    sums = totals(sums, sizes, nz, 7)
+    sums, grad_embed, grad_out, grad_hidden, mask = finish(
+        sums, four(dtok), mask, normed, grad_out, grad_hidden, srcs, sizes, nz, 5
+    )
     grad_qkv, grad_proj = plain(
         unpack_body,
         [jax.ShapeDtypeStruct(w_qkv.shape, F32), jax.ShapeDtypeStruct(w_proj.shape, F32)],
@@ -636,11 +789,11 @@
     )(sums)
     return (
         mask.reshape(frames, cols),
-        both_cores(grad_embed),
+        interleaved(grad_embed),
         grad_qkv,
         grad_proj,
-        both_cores(grad_hidden),
-        both_cores(grad_out),
+        interleaved(grad_hidden),
+        interleaved(grad_out),
     )
 
 

time: 328 us -> 212 us (0.65)
  waiting for transfers between devices: 35.6 us -> 0 us
  Pallas kernels: 223 us -> 192 us
  local copies, waits for them, and re-layouts: 40.8 us -> 17.6 us
  starting transfers between devices: 16.1 us -> 0 us
  other arithmetic: 9.89 us -> 0.01 us
    pallas_call x7 -> x4, Pallas kernels: 114 us -> 64.1 us  [exchange(): pl.pallas_call(functools.partial(exchange_body, nx, ny, cores, count), ou...]
    pallas_call x2, Pallas kernels: 41.6 us -> 80.4 us  [the longest x1 52.2 us: finish(): pl.pallas_call(functools.partial(finish_body, nx, ny, nz), out_shape=[jax...]
    ppermute x21 -> x0, waiting for transfers between devices: 35.6 us -> none  [the longest x3 10.9 us: summed_over_z(): one_up = lax.ppermute(piece(2, 1), 'z', up)]
    unnamed x65 -> x24, local copies, waits for them, and re-layouts: 27.7 us -> 5.48 us
    ppermute x21 -> x0, starting transfers between devices: 16.1 us -> none  [the longest x3 3.36 us: summed_over_z(): one_down = lax.ppermute(piece(2, 0), 'z', down)]
    another operation x6 -> x0, other arithmetic: 6.4 us -> none
    pallas_call x1, Pallas kernels: 7.78 us -> 3.13 us  [band_tiles(): plain(tiles_body, [tile, tile, ints, ints], [VMEM, VMEM, SMEM, SMEM], [pl...]
    dynamic_slice x3 -> x0, local copies, waits for them, and re-layouts: 4.38 us -> none  [piece(): lax.dynamic_slice(grads, (half * (slots // 2), at, 0), (slots // 2, part,...]
  transfers between devices with their start and end apart: 21 -> 0, of which waited for: 9 -> 0; matrix products, arithmetic and copies ran while one was open for 5% -> 0% of each run, Pallas kernels for 18% -> 0%
where the time goes in v2:
time: 212 us; the launch traced here: 211 us
  Pallas kernels  192 us (91%)
  local copies, waits for them, and re-layouts  17.6 us (8%)
    pallas_call x4, Pallas kernels, exchange(): pl.pallas_call(functools.partial(exchange_body, nx, ny, cores, count), ou...  64.1 us
    pallas_call x1, Pallas kernels, finish(): pl.pallas_call(functools.partial(finish_body, nx, ny, nz), out_shape=[jax...  52.2 us
    pallas_call x1, Pallas kernels, spread(): pl.pallas_call(functools.partial(spread_body, *sizes, nz), out_shape=out,...  28.3 us
    pallas_call x1, Pallas kernels, attention_forward(): plain(forward_body, [jax.ShapeDtypeStruct(tokens.shape, BF16), jax.ShapeD...  14.4 us
    pallas_call x1, Pallas kernels, attention_backward(): plain(backward_body, [jax.ShapeDtypeStruct(grads.shape, BF16), jax.ShapeD...  12.8 us
    pallas_call x1, Pallas kernels, tail(): pl.pallas_call(tail_body, grid=(slots,), out_shape=[jax.ShapeDtypeStruct(...  11.9 us
    dynamic_slice x3, local copies, waits for them, and re-layouts, own(): return lax.dynamic_slice_in_dim(w, c * pair, pair, 1).transpose(1, 0, 2)  8.69 us
    unnamed x24, local copies, waits for them, and re-layouts  5.48 us

profile of v2, /device:TPU:0, one launch (start us, length us, event | category | flops | bytes accessed | tf_op | source)
XLA Modules:
  0.0 210.6 jit_solution(5045148622262587616)
XLA Ops:
  0.6 0.0 copy-start
  0.7 0.0 copy-start.3
  0.7 1.0 copy-done.3
  1.6 0.0 copy-start.4
  1.6 0.9 copy-done.4
  2.5 11.3 %shard_map.136 = (bf16[16,16,256]{2,1,0:T(8,128)(2,1)S(1)}, bf16[16,16,256]{2,1,0:T(8,128)(2,1)S(1)}) custom-call(bf16[16,16,256]{2,1,0:T(8,128)(2,1)S(1)} %bitcast.43, bf16[16,16,256]{2,1,0:T(8,128)(2,1)S(1)} %bitcast.44), custom_call_target="tpu_custom_call" | custom-call | tf_op jit(solution)/shard_map/pallas_call | solution.py:83
  13.8 0.0 copy-done
  13.8 0.4 constant_dynamic-slice_fusion.2
  14.3 0.0 copy-start.5
  14.3 0.6 copy-done.5
  14.9 0.0 copy-start.7
  14.9 0.7 copy-done.7
  15.6 3.1 %shard_map.137 = (bf16[64,16,256]{2,1,0:T(8,128)(2,1)S(1)}, bf16[64,16,256]{2,1,0:T(8,128)(2,1)S(1)}, s32[32]{0:T(128)S(1)}, s32[32]{0:T(128)S(1)}) custom-call(bf16[16,16,256]{2,1,0:T(8,128)(2,1)S(1)} %get-tuple-element.38.spec_ref, bf16[16,16,256]{2,1,0:T(8,128)(2,1)S(1)} %get-tuple-element.39.cot_ref, s32[32]{0:T(128)S(1)} %copy-done.5, s32[32]{0:T(128)S(1)} %copy-done.7), custom_call_target="tpu_custom_call" | custom-call | tf_op jit(solution)/shard_map/pallas_call | solution.py:153
  18.7 19.1 %shard_map.138 = (bf16[32,2,16,256]{3,2,1,0:T(8,128)(2,1)S(1)}, bf16[32,2,16,256]{3,2,1,0:T(8,128)(2,1)S(1)}) custom-call(bf16[32,2,16,256]{3,2,1,0:T(8,128)(2,1)S(1)} %bitcast.41, bf16[32,2,16,256]{3,2,1,0:T(8,128)(2,1)S(1)} %bitcast.42), custom_call_target="tpu_custom_call" | custom-call | tf_op jit(solution)/shard_map/pallas_call | solution.py:83
  37.8 0.0 slice-start
  37.9 0.4 shard_map.139.refs_0_
  38.3 16.1 %shard_map.140 = bf16[32,2,16,384]{3,2,1,0:T(8,128)(2,1)S(1)} custom-call(bf16[32,2,16,384]{3,2,1,0:T(8,128)(2,1)S(1)} %shard_map.139.refs_0_), custom_call_target="tpu_custom_call" | custom-call | tf_op jit(solution)/shard_map/pallas_call | solution.py:83
  54.4 0.0 slice-start.1
  54.4 4.9 %constant_dynamic-slice_fusion.1 = bf16[384,2,1536]{2,1,0:T(2,128)(2,1)S(1)} fusion(bf16[384,4,1536]{2,1,0:T(4,128)(2,1)} %param.16, s32[]{:T(128)S(6)} %select_n.2), kind=kLoop, calls=%fused_computation.7 | loop fusion | bytes 4718596 | tf_op jit(solution)/shard_map/dynamic_slice | solution.py:763
  59.4 0.2 copy.31
  59.6 0.0 slice-done
  59.6 0.0 slice-done.1
  59.6 3.4 %constant_dynamic-slice_fusion = bf16[1536,2,512]{2,1,0:T(2,128)(2,1)S(1)} fusion(bf16[1536,4,512]{2,1,0:T(4,128)(2,1)S(1)} %bitcast.48, s32[]{:T(128)S(6)} %select_n.2), kind=kLoop, calls=%fused_computation.6 | loop fusion | bytes 6291460 | tf_op jit(solution)/shard_map/dynamic_slice | solution.py:763
  63.0 0.0 copy-start.1
  63.0 0.0 copy-start.2
  63.0 0.5 copy.30
  63.5 0.7 copy-done.1
  64.3 0.1 copy-done.2
  64.4 14.4 %shard_map.141 = (bf16[64,16,384]{2,1,0:T(8,128)(2,1)S(1)}, bf16[512,384]{1,0:T(8,128)(2,1)S(1)}, bf16[512,1536]{1,0:T(8,128)(2,1)S(1)}, f32[8,512,128]{2,1,0:T(8,128)S(1)}, bf16[512,512]{1,0:T(8,128)(2,1)S(1)}) custom-call(bf16[64,16,384]{2,1,0:T(8,128)(2,1)S(1)} %bitcast.33, s32[32]{0:T(128)S(1)} %get-tuple-element.43.slots_ref, ...), custom_call_target="tpu_custom_call" | custom-call | tf_op jit(solution)/shard_map/pallas_call | solution.py:285
  78.7 17.6 %shard_map.142.mixed_ref = bf16[32,2,16,384]{3,2,1,0:T(8,128)(2,1)S(1)} custom-call(bf16[32,2,16,384]{3,2,1,0:T(8,128)(2,1)S(1)} %bitcast.37), custom_call_target="tpu_custom_call" | custom-call | tf_op jit(solution)/shard_map/pallas_call | solution.py:83
  96.3 11.9 %shard_map.143 = (bf16[32,2,16,256]{3,2,1,0:T(8,128)(2,1)S(1)}, bf16[32,2,16,384]{3,2,1,0:T(8,128)(2,1)S(1)}, bf16[2,384,1536]{2,1,0:T(8,128)(2,1)S(1)}, bf16[2,1536,512]{2,1,0:T(8,128)(2,1)S(1)}) custom-call(bf16[32,2,16,384]{3,2,1,0:T(8,128)(2,1)S(1)} %shard_map.142.mixed_ref, bf16[32,2,16,256]{3,2,1,0:T(8,128)(2,1)S(1)} %get-tuple-element.45.cot_ref, ...), custom_call_target="tpu_custom_call" | custom-call | tf_op jit(solution)/shard_map/pallas_call | solution.py:444
  108.2 28.3 %shard_map.144 = (bf16[32,2,16,384]{3,2,1,0:T(8,128)(2,1)S(1)}, bf16[32,2,16,256]{3,2,1,0:T(8,128)(2,1)S(1)}, bf16[384,512]{1,0:T(8,128)(2,1)S(1)}, bf16[384,512...) custom-call(bf16[32,2,16,384]{3,2,1,0:T(8,128)(2,1)S(1)} %get-tuple-element.46.refs_0_, ...), custom_call_target="tpu_custom_call" | custom-call | tf_op jit(solution)/shard_map/pallas_call | solution.py:553
  136.5 0.0 copy-start.6
  136.5 12.8 %shard_map.145 = (bf16[64,16,384]{2,1,0:T(8,128)(2,1)S(1)}, bf16[32,64,384]{2,1,0:T(8,128)(2,1)S(1)}) custom-call(bf16[64,16,384]{2,1,0:T(8,128)(2,1)S(1)} %bitcast.38, s32[32]{0:T(128)S(1)} %get-tuple-element.43.slots_ref, bf16[384,1536]{1,0:T(8,128)(2,1)S(1)} %copy-done.1, bf16[512,384]{1,0:T(8,128)(2,1)S(1)} %copy-done.2, ...), custom_call_target="tpu_custom_call" | custom-call | tf_op jit(solution)/shard_map/pallas_call | solution.py:365
  149.3 0.0 copy-done.6
  149.3 3.2 %shard_map.146.refs_2_ = bf16[16,16,256]{2,1,0:T(8,128)(2,1)S(1)} custom-call(bf16[64,16,256]{2,1,0:T(8,128)(2,1)S(1)} %bitcast.40, s32[32]{0:T(128)S(1)} %copy-done.6, s32[32]{0:T(128)S(1)} %get-tuple-element.58.starts_ref, s32[32]{0:T(128)S(1)} %get-tuple-element.43.slots_ref), custom_call_target="tpu_custom_call" | custom-call | tf_op jit(solution)/shard_map/pallas_call | solution.py:185
  152.5 52.2 %shard_map.147 = (bf16[32,64,384]{2,1,0:T(8,128)(2,1)S(1)}, bf16[2,2,32,384]{3,2,1,0:T(8,128)(2,1)S(1)}, bf16[2,2,192,512]{3,2,1,0:T(8,128)(2,1)S(1)}, bf16[2,2,...) custom-call(bf16[32,64,384]{2,1,0:T(8,128)(2,1)S(1)} %get-tuple-element.55.refs_0_, ...), custom_call_target="tpu_custom_call" | custom-call | tf_op jit(solution)/shard_map/pallas_call | solution.py:735
  204.7 0.7 copy.35
  205.4 1.3 copy.33
  206.7 1.5 copy.32
  208.2 1.8 shard_map.148
  210.0 0.7 copy.37
  (2 shorter events, 0.0 us)
Async XLA Ops:
  0.6 13.2 %copy-start = (bf16[256,4,384]{2,1,0:T(4,128)(2,1)S(1)}, bf16[256,4,384]{2,1,0:T(4,128)(2,1)}, u32[]{:S(2)}) copy-start(bf16[256,4,384]{2,1,0:T(4,128)(2,1)} %param.13) | copy-start | bytes 2359300
  0.7 1.0 copy-start.3
  1.6 0.9 copy-start.4
  14.3 0.7 copy-start.5
  14.9 0.7 copy-start.7
  37.8 21.8 %slice-start = ((s8[6291456]{0:T(1024)(128)(4,1)}), s8[4194304]{0:T(1024)(128)(4,1)S(1)}, s32[]{:S(2)}) async-start(s8[6291456]{0:T(1024)(128)(4,1)} %bitcast.47), calls=%async_computation | async-start | bytes 8388608
  54.4 5.2 %slice-start.1 = ((s8[6291456]{0:T(1024)(128)(4,1)}), s8[2097152]{0:T(1024)(128)(4,1)S(1)}, s32[]{:S(2)}) async-start(s8[6291456]{0:T(1024)(128)(4,1)} %bitcast.47), calls=%async_computation.1 | async-start | bytes 4194304
  63.0 1.3 copy-start.1
  63.0 1.3 copy-start.2
  136.5 12.9 %copy-start.6 = (s32[32]{0:T(128)S(1)}, s32[32]{0:T(128)}, u32[]{:S(2)}) copy-start(s32[32]{0:T(128)} %widths_ref.3) | copy-start | bytes 388

commit v3 on v0

v3 whole, which is shorter than its diff:
```python
import functools

import jax
import jax.numpy as jnp
from jax import lax
from jax.experimental import pallas as pl
from jax.experimental.pallas import tpu as pltpu
from jax.sharding import Mesh
from jax.sharding import PartitionSpec as P

HEAD_DIM = 64
EPSILON = 1e-05
MESH = pl.DeviceIdType.MESH
BF16 = jnp.bfloat16
F32 = jnp.float32
VMEM = pl.BlockSpec(memory_space=pltpu.VMEM)
SMEM = pl.BlockSpec(memory_space=pltpu.SMEM)
ANY = pl.BlockSpec(memory_space=pl.ANY)
MIB = 1024 * 1024
BLOCK = 128
FAR_AWAY = 1 << 20


def dot(a, b, da, db):
    return lax.dot_general(a, b, (((da,), (db,)), ((), ())), preferred_element_type=F32)


TABLE = 64
SLOT, START, COLUMNS, OFFSET, SLOT_BAND, SLOT_COLUMNS, SLOT_BASE, SLOT_OFFSET, PICK = (TABLE * i for i in range(9))


def tables_body(groups, slot_count, blocks, widths_ref, group_ref, out_ref, counts):
    bands = widths_ref.shape[0]

    def clear(j, carry):
        out_ref[START + j] = FAR_AWAY
        for row in (SLOT, COLUMNS, OFFSET, SLOT_BAND, SLOT_COLUMNS, SLOT_BASE, SLOT_OFFSET):
            out_ref[row + j] = 0
        return carry

    lax.fori_loop(0, TABLE, clear, 0)
    for g in range(groups):
        counts[g] = 0

    def index(b, start):
        group = group_ref[b]
        width = widths_ref[b]
        rank = counts[group]
        counts[group] = rank + 1
        slot = group * slot_count + rank
        out_ref[SLOT + b] = slot
        out_ref[START + b] = start
        out_ref[COLUMNS + b] = 4 * width
        out_ref[OFFSET + b] = 4 * (start % 32)
        out_ref[SLOT_BAND + slot] = b
        out_ref[SLOT_COLUMNS + slot] = 4 * width
        out_ref[SLOT_BASE + slot] = start // 32
        out_ref[SLOT_OFFSET + slot] = 4 * (start % 32)
        return start + width

    lax.fori_loop(0, bands, index, jnp.int32(0))

    def locate(i, b):
        for _ in range(2):
            b = b + jnp.where(out_ref[START + b + 1] <= 32 * i, 1, 0)
        for r in range(3):
            start = out_ref[START + b + r]
            inside = (start < 32 * i + 32) & (i - start // 32 < 3)
            out_ref[PICK + 3 * i + r] = jnp.where(inside, 3 * (b + r) + i - start // 32, 3 * bands)
        return b

    lax.fori_loop(0, blocks, locate, jnp.int32(0))


def tables(widths, band_group, groups, slot_count, blocks):
    return pl.pallas_call(
        functools.partial(tables_body, groups, slot_count, blocks),
        out_shape=jax.ShapeDtypeStruct((8 * TABLE + 128,), jnp.int32),
        in_specs=[SMEM, SMEM],
        out_specs=SMEM,
        scratch_shapes=[pltpu.SMEM((groups,), jnp.int32)],
    )(widths, band_group)


def remote(src, dst, send, recv, where):
    return pltpu.make_async_remote_copy(
        src_ref=src, dst_ref=dst, send_sem=send, recv_sem=recv, device_id=where, device_id_type=MESH
    )


def shift(axis, step, size):
    return lax.rem(lax.axis_index(axis) + step + size, size)


def steps_in_plane(nx, ny, cores):
    def hops(d):
        return min(d[0], nx - d[0]) + min(d[1], ny - d[1])

    every = [(i, j, k) for i in range(nx) for j in range(ny) for k in range(cores)]
    return sorted(every[1:], key=lambda d: -hops(d))


def target(d, nx, ny):
    x, y, c = shift("x", d[0], nx), shift("y", d[1], ny), shift("c", d[2], 2)
    chip = x * ny + y
    return {"x": x, "y": y, "c": c}, chip, chip * 2 + c


def rows_of(ref, slot, step, nz):
    part = ref.shape[1] // nz
    return ref.at[slot, pl.ds(pl.multiple_of(shift("z", step, nz) * part, part), part)]


def z_place(step, nz):
    return {"z": shift("z", step, nz)}


class Flight:
    def __init__(self, copies):
        self.copies = copies
        for copy in copies:
            copy.start()

    def recv(self):
        for copy in self.copies:
            copy.wait_recv()

    def send(self):
        for copy in self.copies:
            copy.wait_send()


class Ring:
    def __init__(self, grad, bufs, send, recv, nz):
        self.grad, self.nz, self.s, self.r = grad, nz, send, recv
        self.far, self.src, self.near, self.side = bufs
        self.flights = []

    def go(self, copies):
        self.flights.append(Flight(copies))
        return self.flights[-1]

    def first(self, slot):
        step = -1 if slot == 0 else 1
        self.go([
            remote(rows_of(self.grad, slot, 2, self.nz), self.far.at[slot], self.s.at[0, slot], self.r.at[0, slot], z_place(step, self.nz)),
            remote(rows_of(self.grad, slot, -step, self.nz), self.side.at[slot], self.s.at[1, slot], self.r.at[1, slot], z_place(-step, self.nz)),
        ])

    def second(self):
        for slot in range(2):
            step = -1 if slot == 0 else 1
            self.flights[slot].copies[0].wait_recv()
            mine = rows_of(self.grad, slot, step, self.nz)[...]
            self.src[slot] = (self.far[slot].astype(F32) + mine.astype(F32)).astype(BF16)
            self.go([remote(self.src.at[slot], self.near.at[slot], self.s.at[2, slot], self.r.at[2, slot], z_place(step, self.nz))])

    def finish(self, halves, swap, send, recv):
        ci = lax.axis_index("c")
        half = halves.shape[2]
        for slot in range(2):
            self.flights[slot].copies[1].wait_recv()
            self.flights[2 + slot].recv()
            mine = rows_of(self.grad, slot, 0, self.nz)[...].astype(F32)
            rows = (mine + self.near[slot].astype(F32) + self.side[slot].astype(F32)).astype(BF16)
            low, high = rows[:half], rows[half:]
            halves[ci, slot] = jnp.where(ci == 0, low, high)
            swap[slot] = jnp.where(ci == 0, high, low)
        return self.go([remote(swap, halves.at[ci], send, recv, {"c": 1 - ci})])

    def end(self):
        for flight in self.flights:
            flight.send()


def moved(rows, offset, left):
    window = rows.shape[1]
    bits = jnp.full(rows.shape, offset, jnp.int32)
    for bit in (4, 8, 16, 32, 64):
        rows = jnp.where((bits & bit) != 0, pltpu.roll(rows, window - bit if left else bit, 1), rows)
    return rows


def band_window(blocks, info, j, feat):
    base = info[SLOT_BASE + j]
    raw = jnp.concatenate([blocks[base + i] for i in range(feat // 128 + 1)], axis=1)
    rows = moved(raw, info[SLOT_OFFSET + j], True)[:, :feat]
    lane = lax.broadcasted_iota(jnp.int32, rows.shape, 1)
    return jnp.where(lane < info[SLOT_COLUMNS + j], rows, 0.0)


def normed_tile(blocks, info, j, feat):
    raw = band_window(blocks, info, j, feat)
    counted = jnp.maximum(jnp.full((raw.shape[0], 1), info[SLOT_COLUMNS + j], jnp.int32), 1).astype(F32)
    mean = jnp.sum(raw * raw, axis=1, keepdims=True) / counted
    return (raw * lax.rsqrt(mean + EPSILON)).astype(BF16)


def permutation(rows, frames, bands, to_frames):
    a = lax.broadcasted_iota(jnp.int32, (rows, rows), 0)
    b = lax.broadcasted_iota(jnp.int32, (rows, rows), 1)
    if not to_frames:
        a, b = b, a
    return ((a // bands == b % frames) & (a % bands == b // frames)).astype(F32).astype(BF16)


def gather_bands(src, info, stage):
    for b in range(stage.shape[0]):
        stage[b] = src[info[SLOT + b]]


def scatter_slots(stage, info, dst):
    _, pair, frames, width = dst.shape

    def step(p, carry):
        for s in range(pair):
            j = p * pair + s
            live = jnp.full((frames, width), info[SLOT_COLUMNS + j], jnp.int32) > 0
            dst[p, s] = jnp.where(live, stage[info[SLOT_BAND + j]].astype(F32), 0.0).astype(BF16)
        return carry

    lax.fori_loop(0, dst.shape[0], step, 0, unroll=4)


def attention_forward(tok, info, w_qkv, w_proj, dst, rows_ref, packed, soft_ref, heads_ref, stage):
    bands, frames, width = stage.shape
    rows = bands * frames
    inner = w_proj.shape[0]
    heads = inner // HEAD_DIM
    gather_bands(tok, info, stage)
    tokens32 = dot(permutation(rows, frames, bands, True), stage[...].reshape(rows, width), 1, 0)
    rows_ref[...] = tokens32.astype(BF16)
    inv = lax.rsqrt(jnp.mean(tokens32 * tokens32, axis=1, keepdims=True) + EPSILON)
    packed[...] = dot((tokens32 * inv).astype(BF16), w_qkv[...], 1, 0).astype(BF16)
    row_id = lax.broadcasted_iota(jnp.int32, (BLOCK, BLOCK), 0) // bands
    col_id = lax.broadcasted_iota(jnp.int32, (BLOCK, BLOCK), 1) // bands
    same = row_id == col_id

    def step(i, carry):
        at = pl.ds(pl.multiple_of(i * BLOCK, BLOCK), BLOCK)
        outs = []
        for h in range(heads):
            lo = h * HEAD_DIM
            q = packed[at, lo : lo + HEAD_DIM]
            k = packed[at, inner + lo : inner + lo + HEAD_DIM]
            v = packed[at, 2 * inner + lo : 2 * inner + lo + HEAD_DIM]
            scores = jnp.where(same, dot(q, k, 1, 1) * HEAD_DIM ** (-0.5), -jnp.inf)
            expd = jnp.exp(scores - jnp.max(scores, axis=1, keepdims=True))
            soft = expd / jnp.sum(expd, axis=1, keepdims=True)
            soft_ref[h, at, :] = soft
            outs.append(dot(soft.astype(BF16), v, 1, 0))
        heads_ref[at, :] = jnp.concatenate(outs, axis=1).astype(BF16)
        return carry

    lax.fori_loop(0, rows // BLOCK, step, 0)
    mixed = (rows_ref[...].astype(F32) + dot(heads_ref[...], w_proj[...], 1, 0)).astype(BF16)
    back = dot(permutation(rows, frames, bands, False), mixed, 1, 0).astype(BF16)
    stage[...] = back.reshape(bands, frames, width)
    scatter_slots(stage, info, dst)


def attention_scores_backward(grad, info, w_proj, packed, soft_ref, stage, grads_ref, dheads, dpacked):
    bands, frames, width = stage.shape
    rows = bands * frames
    inner = w_proj.shape[0]
    heads = inner // HEAD_DIM
    gather_bands(grad, info, stage)
    grads_ref[...] = dot(permutation(rows, frames, bands, True), stage[...].reshape(rows, width), 1, 0).astype(BF16)
    dheads[...] = dot(grads_ref[...], w_proj[...], 1, 1).astype(BF16)

    def step(i, carry):
        at = pl.ds(pl.multiple_of(i * BLOCK, BLOCK), BLOCK)
        dq, dk, dv = [], [], []
        for h in range(heads):
            lo = h * HEAD_DIM
            q = packed[at, lo : lo + HEAD_DIM]
            k = packed[at, inner + lo : inner + lo + HEAD_DIM]
            v = packed[at, 2 * inner + lo : 2 * inner + lo + HEAD_DIM]
            g = dheads[at, lo : lo + HEAD_DIM]
            soft = soft_ref[h, at, :]
            p_grad = dot(g, v, 1, 1)
            dv.append(dot(soft.astype(BF16), g, 0, 0))
            around = soft * (p_grad - jnp.sum(p_grad * soft, axis=1, keepdims=True))
            around = (around * HEAD_DIM ** (-0.5)).astype(BF16)
            dq.append(dot(around, k, 1, 0))
            dk.append(dot(around, q, 0, 0))
        dpacked[at, :] = jnp.concatenate(dq + dk + dv, axis=1).astype(BF16)
        return carry

    lax.fori_loop(0, rows // BLOCK, step, 0)


def attention_sums(rows_ref, heads_ref, grads_ref, dpacked, sums):
    pieces, depth, width = sums.shape
    inner = heads_ref.shape[1]
    small = inner // pieces
    tall = depth - small
    across = 3 * inner // width
    proj = dot(heads_ref[...], grads_ref[...], 0, 0).astype(BF16)
    sums[:, tall:, :] = proj.reshape(pieces, small, width)
    tokens32 = rows_ref[...].astype(F32)
    inv = lax.rsqrt(jnp.mean(tokens32 * tokens32, axis=1, keepdims=True) + EPSILON)
    normed = (tokens32 * inv).astype(BF16)
    for j in range(across):
        part = dot(normed, dpacked[:, j * width : (j + 1) * width], 0, 0).astype(BF16)
        for i in range(pieces // across):
            sums[i * across + j, :tall, :] = part[i * tall : (i + 1) * tall, :]


def attention_tokens_backward(info, w_qkv, rows_ref, grads_ref, dpacked, stage, dst):
    bands, frames, width = stage.shape
    rows = bands * frames
    tokens32 = rows_ref[...].astype(F32)
    inv = lax.rsqrt(jnp.mean(tokens32 * tokens32, axis=1, keepdims=True) + EPSILON)
    normed32 = tokens32 * inv
    gn = dot(dpacked[...], w_qkv[...], 1, 1)
    back = grads_ref[...].astype(F32) + inv * (gn - normed32 * jnp.mean(gn * normed32, axis=1, keepdims=True))
    back = dot(permutation(rows, frames, bands, False), back.astype(BF16), 1, 0).astype(BF16)
    stage[...] = back.reshape(bands, frames, width)
    scatter_slots(stage, info, dst)


def mask_assembly(tiles, info, shifted, out):
    parts, frames, cols = out.shape
    feat = tiles.shape[2]
    bands = (shifted.shape[0] - 1) // 3
    lane = lax.broadcasted_iota(jnp.int32, (frames, feat), 1)
    shifted[3 * bands] = jnp.zeros((frames, 128), F32)

    def shift_band(b, carry):
        tile = jnp.where(lane < info[COLUMNS + b], tiles[info[SLOT + b]].astype(F32), 0.0)
        wide = moved(jnp.concatenate([tile, jnp.zeros((frames, 128), F32)], axis=1), info[OFFSET + b], False)
        for m in range(3):
            shifted[3 * b + m] = wide[:, m * 128 : (m + 1) * 128]
        return carry

    lax.fori_loop(0, bands, shift_band, 0, unroll=4)

    def step(p, carry):
        for half in range(cols // 128):
            i = 3 * (p * (cols // 128) + half)
            total = shifted[info[PICK + i]] + shifted[info[PICK + i + 1]] + shifted[info[PICK + i + 2]]
            out[p, :, half * 128 : (half + 1) * 128] = total.astype(BF16)
        return carry

    lax.fori_loop(0, parts, step, 0, unroll=4)


def tail_slot(s, mixed, cots, wh, wo, mask_ref, dmix_ref, gh, go, normed, hidden, dout, dpre):
    peers, _, frames, width = mixed.shape
    feat = cots.shape[3]
    rows = peers * frames
    chunk = min(rows, 256)
    lump = chunk // frames

    def step(i, carry):
        at = pl.ds(pl.multiple_of(i * chunk, chunk), chunk)
        who = pl.ds(i * lump, lump)
        x = mixed[who, s].reshape(chunk, width).astype(F32)
        inv = lax.rsqrt(jnp.mean(x * x, axis=1, keepdims=True) + EPSILON)
        n = x * inv
        nb = n.astype(BF16)
        normed[at, :] = nb
        t = jnp.tanh(dot(nb, wh[s], 1, 0))
        hb = t.astype(BF16)
        hidden[at, :] = hb
        out = dot(hb, wo[s], 1, 0)
        value = out[:, :feat]
        gate = jax.nn.sigmoid(out[:, feat:])
        mask_ref[who, s] = (value * gate).astype(BF16).reshape(lump, frames, feat)
        c = cots[who, s].reshape(chunk, feat).astype(F32)
        cg = c * gate
        g = jnp.concatenate([cg, cg * value * (1.0 - gate)], axis=1).astype(BF16)
        dout[at, :] = g
        gp = (dot(g, wo[s], 1, 1) * (1.0 - t * t)).astype(BF16)
        dpre[at, :] = gp
        gn = dot(gp, wh[s], 1, 1)
        dm = inv * (gn - n * jnp.mean(gn * n, axis=1, keepdims=True))
        dmix_ref[who, s] = dm.astype(BF16).reshape(lump, frames, width)
        return carry

    lax.fori_loop(0, rows // chunk, step, 0)


def tail_weights(s, gh, go, normed, hidden, dout, dpre):
    go[s] = dot(hidden[...], dout[...], 0, 0).astype(BF16)
    gh[s] = dot(normed[...], dpre[...], 0, 0).astype(BF16)


def own_slots(buf, out, first, rows):
    pair = out.shape[0]
    depth = 32

    def part(base):
        def step(i, carry):
            at = pl.ds(pl.multiple_of(i * depth, depth), depth)
            to = pl.ds(pl.multiple_of(first + i * depth, depth), depth)
            for s in range(pair):
                out[s, to, :] = buf[at, base + s, :]
            return carry

        lax.fori_loop(0, rows // depth, step, 0)

    for c in range(2):
        pl.when(lax.axis_index("c") == c)(functools.partial(part, c * pair))


def step_body(nx, ny, nz, names, *refs):
    r = dict(zip(names, refs))
    xi, yi, zi, ci = (lax.axis_index(n) for n in ("x", "y", "z", "c"))
    chips = nx * ny
    me = xi * ny + yi
    who = me * 2 + ci
    info = r["info"]
    other = {"c": 1 - ci}
    every = steps_in_plane(nx, ny, 2)
    alone = steps_in_plane(nx, ny, 1)
    peers, pair, frames, feat = r["normed"].shape

    barrier = pltpu.get_barrier_semaphore()
    for d in every:
        pl.semaphore_signal(barrier, inc=1, device_id=target(d, nx, ny)[0], device_id_type=MESH)
    for k in range(1, nz):
        pl.semaphore_signal(barrier, inc=1, device_id=z_place(k, nz), device_id_type=MESH)
    loads = []
    chunks = {"h": 4, "o": 4}
    for name, count in chunks.items():
        w, buf = r["w" + name + "_hbm"], r["w" + name + "_buf"]
        rows = w.shape[0] // count
        loads.append([
            pltpu.make_async_copy(w.at[pl.ds(i * rows, rows)], buf.at[i % 2], r["load_sem"].at[len(loads), i])
            for i in range(count)
        ])

    def take(index, name):
        copies = loads[index]
        buf, out = r["w" + name + "_buf"], r["w" + name]
        rows = buf.shape[1]
        for i, copy in enumerate(copies):
            copy.wait()
            own_slots(buf.at[i % 2], out, i * rows, rows)
            if i + 2 < len(copies):
                copies[i + 2].start()

    for copies in loads:
        copies[0].start()
        copies[1].start()
    ends = []

    def same_core(src, dst, job):
        out = []
        for k, d in enumerate(alone):
            where, chip, _ = target(d, nx, ny)
            out.append(remote(src.at[chip], dst.at[me], r["chip_s"].at[job, k], r["chip_r"].at[job, k], where))
        ends.append(Flight(out))
        return ends[-1]

    def piece(ref, place, slot=None):
        if len(ref.shape) == 4:
            return ref.at[place] if slot is None else ref.at[place, slot]
        return ref.at[pl.ds(place * pair, pair)] if slot is None else ref.at[place * pair + slot]

    def to_all(src, dst, job, slot=None, group=None):
        out = []
        for k, d in enumerate(every):
            if group is not None and d[0] != group:
                continue
            where, _, peer = target(d, nx, ny)
            a, b = piece(src, peer, slot), piece(dst, who, slot)
            out.append(remote(a, b, r["all_s"].at[job, k], r["all_r"].at[job, k], where))
        ends.append(Flight(out))
        return ends[-1]

    def keep(src, dst, index, job):
        a, b = (src.at[index], dst.at[index]) if src.shape == r["spec"].shape else (piece(src, index), piece(dst, index))
        copy = pltpu.make_async_copy(a, b, r["keep_sem"].at[job])
        copy.start()
        return copy

    pl.semaphore_wait(barrier, len(every) + nz - 1)

    got_spec = same_core(r["spec"], r["spec_rx"], 0)
    got_cot = same_core(r["cot"], r["cot_rx"], 1)
    kept = [keep(r["spec"], r["spec_rx"], me, 0), keep(r["cot"], r["cot_rx"], me, 1)]
    per = r["spec"].shape[2] // 128
    blocks = (r["spec_blocks"], r["cot_blocks"])
    for b in blocks:
        b[chips * per :] = jnp.zeros((b.shape[0] - chips * per, frames, 128), F32)
    take(1, "o")
    for which, (got, rx) in enumerate(((got_spec, r["spec_rx"]), (got_cot, r["cot_rx"]))):
        got.recv()
        kept[which].wait()
        for p in range(chips):
            for i in range(per):
                blocks[which][p * per + i] = rx[p, :, i * 128 : (i + 1) * 128].astype(F32)
        if which:
            break
        got_normed = []
        for group in sorted(range(nx), key=lambda g: -min(g, nx - g)):
            row = shift("x", group, nx) * ny * 2

            def tile(p, carry):
                for s in range(2):
                    r["normed_tx"][row + p, s] = normed_tile(blocks[0], info, (row + p) * 2 + s, feat)
                return carry

            lax.fori_loop(0, ny * 2, tile, 0, unroll=4)
            got_normed.append(to_all(r["normed_tx"], r["normed"], 0, group=group))
        kept.append(keep(r["normed_tx"], r["normed"], who, 2))

    def cot_tile(p, carry):
        for s in range(2):
            r["cots_tx"][p, s] = band_window(blocks[1], info, p * 2 + s, feat).astype(BF16)
        return carry

    lax.fori_loop(0, chips * 2, cot_tile, 0, unroll=2)
    take(0, "h")
    for flight in got_normed:
        flight.recv()
    kept[2].wait()
    for s in range(pair):
        rows = r["normed"][:, s].reshape(peers * frames, feat)
        r["emb_tx"][:, s] = dot(rows, r["w_embed"][s], 1, 0).astype(BF16).reshape(peers, frames, -1)
    got_tokens = to_all(r["emb_tx"], r["tokens"], 1)
    got_cots = to_all(r["cots_tx"], r["cots"], 2)
    kept = [keep(r["emb_tx"], r["tokens"], who, 0), keep(r["cots_tx"], r["cots"], who, 1)]
    got_tokens.recv()
    kept[0].wait()

    attention_forward(
        r["tokens"], info, r["w_qkv"], r["w_proj"], r["mixed_tx"],
        r["rows"], r["packed"], r["soft"], r["heads"], r["stage"],
    )
    got_mixed = [to_all(r["mixed_tx"], r["mixed"], 3 + s, slot=s) for s in range(pair)]
    mixed_kept = keep(r["mixed_tx"], r["mixed"], who, 2)
    got_cots.recv()
    kept[1].wait()
    mixed_kept.wait()

    ring_o = Ring(r["go"], [r["o_" + n] for n in ("far", "src", "near", "side")], r["ring_s"].at[0], r["ring_r"].at[0], nz)
    ring_h = Ring(r["gh"], [r["h_" + n] for n in ("far", "src", "near", "side")], r["ring_s"].at[1], r["ring_r"].at[1], nz)
    ring_e = Ring(r["ge"], [r["e_" + n] for n in ("far", "src", "near", "side")], r["ring_s"].at[2], r["ring_r"].at[2], nz)
    mine = [r["t_normed"], r["t_hidden"], r["t_dout"], r["t_dpre"]]
    got_dmix = []
    for s in range(pair):
        got_mixed[s].recv()
        tail_slot(s, r["mixed"], r["cots"], r["wh"], r["wo"], r["tiles_tx"], r["dmix_tx"], r["gh"], r["go"], *mine)
        got_dmix.append(to_all(r["dmix_tx"], r["dmix"], 5 + s, slot=s))
        tail_weights(s, r["gh"], r["go"], *mine)
        ring_o.first(s)
        ring_h.first(s)
    kept = [keep(r["dmix_tx"], r["dmix"], who, 0), keep(r["tiles_tx"], r["tiles"], who, 1)]
    got_tiles = to_all(r["tiles_tx"], r["tiles"], 7)
    for flight in got_dmix:
        flight.recv()
    kept[0].wait()
    attention_scores_backward(
        r["dmix"], info, r["w_proj"], r["packed"], r["soft"], r["stage"], r["grads"], r["dheads"], r["dpacked"]
    )
    x_ref, o_ref = r["sums"], r["totals"]
    attention_sums(r["rows"], r["heads"], r["grads"], r["dpacked"], x_ref)

    first = []
    for k, d in enumerate(alone + [(0, 0, 0)]):
        chip = target(d, nx, ny)[1]
        first.append(remote(x_ref.at[(1 - ci) * chips + chip], r["pair"].at[chip], r["pair_s"].at[0, k], r["pair_r"].at[0, k], other))
    ends.append(Flight(first))
    ring_o.second()
    ring_h.second()
    attention_tokens_backward(info, r["w_qkv"], r["rows"], r["grads"], r["dpacked"], r["stage"], r["dtok_tx"])
    landed, part = r["landed"], r["part"]
    to_chips = []
    for k, d in enumerate(alone + [(0, 0, 0)]):
        where, chip, _ = target(d, nx, ny)
        first[k].wait_recv()
        summed = (x_ref[ci * chips + chip].astype(F32) + r["pair"][chip].astype(F32)).astype(BF16)
        if k < len(alone):
            part[chip] = summed
            to_chips.append(Flight([remote(part.at[chip], landed.at[me], r["chip_s"].at[2, k], r["chip_r"].at[2, k], where)]))
        else:
            landed[me] = summed
    ends.extend(to_chips)
    got_dtok = to_all(r["dtok_tx"], r["dtok"], 8)
    kept.append(keep(r["dtok_tx"], r["dtok"], who, 2))
    got_tiles.recv()
    kept[1].wait()
    mask_assembly(r["tiles"], info, r["shifted"], r["mask_tx"])
    got_mask = same_core(r["mask_tx"], r["mask"], 3)
    kept.append(keep(r["mask_tx"], r["mask"], me, 3))
    for flight in to_chips:
        flight.recv()
    total = landed[0].astype(F32)
    for q in range(1, chips):
        total += landed[q].astype(F32)
    deep, final = r["deep"], r["final"]
    r["chip_sum"][...] = total.astype(BF16)
    deep[zi] = total.astype(BF16)
    across = Flight([
        remote(r["chip_sum"], deep.at[zi], r["deep_s"].at[k], r["deep_r"].at[k], z_place(k, nz)) for k in range(1, nz)
    ])
    ends.append(across)
    across.recv()
    total = deep[0].astype(F32)
    for q in range(1, nz):
        total += deep[q].astype(F32)
    final[...] = total.astype(BF16)
    o_ref[ci * chips + me] = total.astype(BF16)
    back = []
    for k, d in enumerate(alone):
        back.append(remote(final, o_ref.at[ci * chips + me], r["chip_s"].at[4, k], r["chip_r"].at[4, k], target(d, nx, ny)[0]))
    ends.append(Flight(back))
    shared = [Flight([remote(final, o_ref.at[ci * chips + me], r["pair_s"].at[1, len(alone)], r["pair_r"].at[1, len(alone)], other)])]

    got_dtok.recv()
    kept[2].wait()
    for s in range(pair):
        left = r["normed"][:, s].reshape(peers * frames, feat)
        right = r["dtok"][:, s].reshape(peers * frames, r["dtok"].shape[3])
        r["ge"][s] = dot(left, right, 0, 0).astype(BF16)
    for s in range(pair):
        ring_e.first(s)
    swaps = [
        ring_o.finish(r["o_half"], r["o_swap"], r["swap_s"].at[0], r["swap_r"].at[0]),
        ring_h.finish(r["h_half"], r["h_swap"], r["swap_s"].at[1], r["swap_r"].at[1]),
    ]
    ring_e.second()
    swaps.append(ring_e.finish(r["e_half"], r["e_swap"], r["swap_s"].at[2], r["swap_r"].at[2]))
    for k, d in enumerate(alone):
        back[k].wait_recv()
        q = ci * chips + target((nx - d[0], ny - d[1], 0), nx, ny)[1]
        shared.append(Flight([remote(o_ref.at[q], o_ref.at[q], r["pair_s"].at[1, k], r["pair_r"].at[1, k], other)]))
    for swap in swaps:
        swap.recv()
    got_mask.recv()
    kept[3].wait()
    for flight in shared:
        flight.recv()
    for flight in ends + shared:
        flight.send()
    for ring in (ring_o, ring_h, ring_e):
        ring.end()
    unpack(o_ref, r["grad_qkv"], r["grad_proj"])


def unpack(sums, qkv, proj):
    pieces, depth, width = sums.shape
    small = proj.shape[0] // pieces
    tall = depth - small
    across = qkv.shape[1] // width
    proj[...] = sums[:, tall:, :].astype(F32).reshape(proj.shape)
    for i in range(pieces // across):
        for j in range(across):
            qkv[i * tall : (i + 1) * tall, j * width : (j + 1) * width] = sums[i * across + j, :tall, :].astype(F32)


def train_step(sizes, info, spec, cot, w_embed, w_qkv, w_proj, w_hidden, w_out):
    nx, ny, nz = sizes
    chips, frames, cols = spec.shape
    peers = 2 * chips
    pair, feat, width = w_embed.shape
    hid, out_cols = w_out.shape[0], w_out.shape[2]
    inner = w_proj.shape[0]
    bands = TABLE // 2
    rows = bands * frames
    many = peers * frames
    pieces = peers
    depth = 4 * inner // pieces
    dma = pltpu.SemaphoreType.DMA

    def vm(*shape):
        return pltpu.VMEM(shape, BF16)

    ins = {
        "info": (info, SMEM), "spec": (spec, VMEM), "cot": (cot, VMEM), "w_embed": (w_embed, VMEM),
        "w_qkv": (w_qkv, VMEM), "w_proj": (w_proj, VMEM), "wh_hbm": (w_hidden, ANY), "wo_hbm": (w_out, ANY),
    }
    dims = {"o": (hid, out_cols), "h": (width, hid), "e": (feat, width)}
    outs = {
        "mask": jax.ShapeDtypeStruct(spec.shape, BF16),
        "grad_qkv": jax.ShapeDtypeStruct(w_qkv.shape, F32),
        "grad_proj": jax.ShapeDtypeStruct(w_proj.shape, F32),
    }
    for n, (a, b) in dims.items():
        outs[n + "_half"] = jax.ShapeDtypeStruct((2, pair, a // nz // 2, b), BF16)
    scratch = {
        "spec_rx": vm(*spec.shape), "cot_rx": vm(*spec.shape),
        "spec_blocks": pltpu.VMEM((chips * cols // 128 + 3, frames, 128), F32),
        "cot_blocks": pltpu.VMEM((chips * cols // 128 + 3, frames, 128), F32),
        "shifted": pltpu.VMEM((3 * bands + 1, frames, 128), F32),
        "wh_buf": vm(2, width // 4, *w_hidden.shape[1:]), "wo_buf": vm(2, hid // 4, *w_out.shape[1:]),
        "wh": vm(pair, width, hid), "wo": vm(pair, hid, out_cols),
        "normed_tx": vm(peers, pair, frames, feat), "normed": vm(peers, pair, frames, feat),
        "cots_tx": vm(peers, pair, frames, feat), "cots": vm(peers, pair, frames, feat),
        "tiles_tx": vm(peers, pair, frames, feat), "tiles": vm(peers * pair, frames, feat),
        "mask_tx": vm(*spec.shape),
        "rows": vm(rows, width), "packed": vm(rows, 3 * inner), "heads": vm(rows, inner),
        "soft": pltpu.VMEM((inner // HEAD_DIM, rows, BLOCK), F32),
        "stage": vm(bands, frames, width), "grads": vm(rows, width), "dheads": vm(rows, inner), "dpacked": vm(rows, 3 * inner),
        "t_normed": vm(many, width), "t_hidden": vm(many, hid), "t_dout": vm(many, out_cols), "t_dpre": vm(many, hid),
        "go": vm(pair, hid, out_cols), "gh": vm(pair, width, hid), "ge": vm(pair, feat, width),
        "sums": vm(pieces, depth, width), "totals": vm(pieces, depth, width),
        "pair": vm(chips, depth, width), "part": vm(chips, depth, width), "landed": vm(chips, depth, width),
        "chip_sum": vm(depth, width), "deep": vm(nz, depth, width), "final": vm(depth, width),
    }
    for n in ("emb_tx", "mixed_tx", "mixed", "dmix_tx", "dtok_tx", "dtok"):
        scratch[n] = vm(peers, pair, frames, width)
    for n in ("tokens", "dmix"):
        scratch[n] = vm(peers * pair, frames, width)
    for n, (a, b) in dims.items():
        for kind in ("far", "src", "near", "side"):
            scratch[n + "_" + kind] = vm(pair, a // nz, b)
        scratch[n + "_swap"] = vm(pair, a // nz // 2, b)
    for n, shape in {
        "load_sem": (2, 4), "keep_sem": (4,), "chip_s": (5, chips), "chip_r": (5, chips), "all_s": (9, peers), "all_r": (9, peers),
        "pair_s": (2, chips), "pair_r": (2, chips), "deep_s": (nz,), "deep_r": (nz,), "ring_s": (3, 3, 2), "ring_r": (3, 3, 2),
        "swap_s": (3,), "swap_r": (3,),
    }.items():
        scratch[n] = dma(shape)
    names = list(ins) + list(outs) + list(scratch)
    results = pl.pallas_call(
        functools.partial(step_body, nx, ny, nz, names),
        out_shape=list(outs.values()),
        in_specs=[spec for _, spec in ins.values()],
        out_specs=[VMEM] * len(outs),
        scratch_shapes=list(scratch.values()),
        compiler_params=pltpu.CompilerParams(collective_id=0, has_side_effects=True, vmem_limit_bytes=63 * MIB),
    )(*[array for array, _ in ins.values()])
    return dict(zip(outs, results))


def interleaved(halves):
    return halves.reshape(-1, *halves.shape[2:]).transpose(1, 0, 2)


def per_device(spec, cotangent, widths, band_group, w_embed, w_qkv, w_proj, w_hidden, w_out):
    frames, cols = spec.shape
    slot_count = w_embed.shape[1]
    sizes = tuple(lax.axis_size(n) for n in ("x", "y", "z"))
    groups = sizes[0] * sizes[1]
    pair = slot_count // 2
    each = frames // groups
    own = lax.dynamic_slice_in_dim(w_embed, lax.axis_index("c") * pair, pair, 1).transpose(1, 0, 2)
    info = tables(widths, band_group, groups, slot_count, groups * cols // 128)
    out = train_step(
        sizes, info, spec.reshape(groups, each, cols), cotangent.reshape(groups, each, cols),
        own, w_qkv, w_proj, w_hidden, w_out,
    )
    return (
        out["mask"].reshape(frames, cols),
        interleaved(out["e_half"]),
        out["grad_qkv"],
        out["grad_proj"],
        interleaved(out["h_half"]),
        interleaved(out["o_half"]),
    )


def solution(mesh):
    split = Mesh(mesh.devices.reshape(4, 4, 4, 2), ("x", "y", "z", "c"))
    band = ("x", "y")
    tm = ("z", "c")
    placed = (
        P(tm, band),
        P(tm, band),
        P(),
        P(),
        P(None, band, None),
        P(),
        P(),
        P(None, band, None),
        P(None, band, None),
    )
    return jax.shard_map(
        per_device,
        mesh=split,
        in_specs=placed,
        out_specs=(
            P(tm, band),
            P(tm, band, None),
            P(),
            P(),
            P(tm, band, None),
            P(tm, band, None),
        ),
        check_vma=False,
    )
```

time: 522 us -> 165 us (0.32); the launches traced: 513 us -> 163 us
  waiting for transfers between devices: 260 us -> 0 us
  Pallas kernels: 0 us -> 151 us
  local copies, waits for them, and re-layouts: 81.6 us -> 11.1 us
  matrix products: 66.6 us -> 0 us
  blocking collectives: 46.4 us -> 0 us
  other arithmetic: 21.4 us -> 0 us
  starting transfers between devices: 19.2 us -> 0 us
  between operations: 17.5 us -> 0.7 us
    psum x1 -> x0, waiting for transfers between devices: 171 us -> none  [packed_total(): subtotal = lax.psum(jnp.concatenate([a.ravel() for a in arrays]), axis)]
    pallas_call x0 -> x2, Pallas kernels: none -> 151 us  [the longest x1 147 us: train_step(): pl.pallas_call(functools.partial(step_body, nx, ny, nz, names), out_shape...]
    dot_general x22 -> x0, matrix products: 62.4 us -> none  [the longest x3 11.3 us: weight_grad(): jnp.einsum('fsa,fsb->asb', left, right, preferred_element_type=jnp.float32)]
    all_gather x1 -> x0, waiting for transfers between devices: 53.6 us -> none  [in_one_piece(): out = lax.all_gather(both, axis, axis=dim, tiled=True)]
    all_to_all x3 -> x0, blocking collectives: 46.4 us -> none  [the longest x1 16.2 us: per_device(): lax.all_to_all(mixed_shards, BAND, split_axis=1, concat_axis=0, tiled=True)]
    all_to_all x4 -> x0, waiting for transfers between devices: 26 us -> none  [the longest x3 13.1 us: sent_and_summed(): lax.all_to_all(cut_along(shard, dim, peers), axis, 0, 0, tiled=True)]
    reshape x13 -> x3, local copies, waits for them, and re-layouts: 27.7 us -> 6.69 us  [interleaved(): return halves.reshape(-1, *halves.shape[2:]).transpose(1, 0, 2)]
    all_to_all x4 -> x0, starting transfers between devices: 19.1 us -> none  [the longest x3 14.1 us: sent_and_summed(): lax.all_to_all(cut_along(shard, dim, peers), axis, 0, 0, tiled=True)]
  transfers between devices with their start and end apart: 8 -> 0, of which waited for: 6 -> 0; matrix products, arithmetic and copies ran while one was open for 15% -> 0% of each run, Pallas kernels for 0% -> 0%
where the time goes in v3:
time: 165 us; the launch traced here: 163 us
  Pallas kernels  151 us (92%)
  local copies, waits for them, and re-layouts  11.1 us (7%)
    pallas_call x1, Pallas kernels, train_step(): pl.pallas_call(functools.partial(step_body, nx, ny, nz, names), out_shape...  147 us
    reshape x3, local copies, waits for them, and re-layouts, interleaved(): return halves.reshape(-1, *halves.shape[2:]).transpose(1, 0, 2)  6.69 us
    pallas_call x1, Pallas kernels, tables(): pl.pallas_call(functools.partial(tables_body, groups, slot_count, blocks)...  4.27 us
    unnamed x12, local copies, waits for them, and re-layouts  4.02 us

profile of v3, /device:TPU:0, one launch (start us, length us, event | category | flops | bytes accessed | tf_op | source)
XLA Modules:
  0.0 162.8 jit_solution(7673408785784419195)
XLA Ops:
  0.6 0.0 copy-start
  0.7 4.3 %shard_map.136.refs_0_ = s32[640]{0:T(1024)} custom-call(s32[32]{0:T(128)} %widths_ref.1, s32[32]{0:T(128)} %group_ref.1), custom_call_target="tpu_custom_call" | custom-call | tf_op jit(solution)/shard_map/pallas_call | solution.py:76
  4.9 0.0 copy-done
  4.9 0.4 constant_dynamic-slice_fusion
  5.4 0.8 copy.26
  6.2 146.7 %shard_map.137 = (bf16[16,16,256]{2,1,0:T(8,128)(2,1)}, f32[384,1536]{1,0:T(8,128)}, f32[512,384]{1,0:T(8,128)}, bf16[2,2,192,512]{3,2,1,0:T(8,128)(2,1)}, bf16[...) custom-call(s32[640]{0:T(1024)} %shard_map.136.refs_0_, bf16[16,16,256]{2,1,0:T(8,128)(2,1)} %bitcast.23, ...), custom_call_target="tpu_custom_call" | custom-call | tf_op jit(solution)/shard_map/pallas_call | solution.py:720
  152.9 0.0 copy-start.3
  152.9 0.0 copy-start.1
  152.9 1.7 %copy.27 = bf16[4,32,384]{2,0,1:T(4,128)(2,1)} copy(bf16[4,32,384]{2,1,0:T(8,128)(2,1)} %bitcast.27) | data formatting | bytes 196608 | tf_op jit(solution)/shard_map/reshape | solution.py:732
  154.7 2.3 %copy.25 = bf16[4,48,1536]{2,0,1:T(4,128)(2,1)} copy(bf16[4,48,1536]{2,1,0:T(8,128)(2,1)} %bitcast.22) | data formatting | bytes 1179648 | tf_op jit(solution)/shard_map/reshape | solution.py:732
  157.0 2.6 %copy.24 = bf16[4,192,512]{2,0,1:T(4,128)(2,1)} copy(bf16[4,192,512]{2,1,0:T(8,128)(2,1)} %bitcast.20) | data formatting | bytes 1572864 | tf_op jit(solution)/shard_map/reshape | solution.py:732
  159.6 0.0 copy-done.3
  159.6 0.7 copy.31
  160.3 0.0 copy-done.1
  160.3 0.0 copy-start.2
  160.3 1.4 copy.32
  161.7 0.3 copy-done.2
  162.0 0.9 copy.33
Async XLA Ops:
  0.6 4.3 %copy-start = (bf16[256,4,384]{2,1,0:T(4,128)(2,1)S(1)}, bf16[256,4,384]{2,1,0:T(4,128)(2,1)}, u32[]{:S(2)}) copy-start(bf16[256,4,384]{2,1,0:T(4,128)(2,1)} %param.13) | copy-start | bytes 2359300
  152.9 6.7 %copy-start.3 = (bf16[16,16,256]{2,1,0:T(8,128)(2,1)S(1)}, bf16[16,16,256]{2,1,0:T(8,128)(2,1)}, u32[]{:S(2)}) copy-start(bf16[16,16,256]{2,1,0:T(8,128)(2,1)} %get-tuple-element.12) | copy-start | bytes 393220
  152.9 7.4 %copy-start.1 = (f32[384,1536]{1,0:T(8,128)S(1)}, f32[384,1536]{1,0:T(8,128)}, u32[]{:S(2)}) copy-start(f32[384,1536]{1,0:T(8,128)} %get-tuple-element.26) | copy-start | bytes 7077892
  160.3 1.7 %copy-start.2 = (f32[512,384]{1,0:T(8,128)S(1)}, f32[512,384]{1,0:T(8,128)}, u32[]{:S(2)}) copy-start(f32[512,384]{1,0:T(8,128)} %get-tuple-element.27) | copy-start | bytes 2359300
